TPU v7x, 32 devices: a whole 2x2x4 slice. The times are simulated.
32 devices in a mesh: section: 2 (over x), grp: 4 (over y, core), dp: 4 (over z).
Axes of the slice: x: 2, y: 2, z: 4, core: 2. Of those that a mesh axis runs over, the one named last changes fastest.
Arguments:
- embeddings: bfloat16 [32, 256, 768], P(('grp', 'dp')), may hold values from -6 to 6
- mask_flags: int32 [32, 256], P(('grp', 'dp')), may hold values 0 or 1
- timesteps: int32 [32], P(('grp', 'dp')), may hold values from 0 to 999, as said below
- time_table: bfloat16 [1000, 768], replicated, may hold values from -6 to 6
- mask_vector: bfloat16 [768], replicated, may hold values from -6 to 6
- attn_qkv: bfloat16 [2, 768, 2304], P('section', 'grp'), may hold values from -0.21875 to 0.21875
- attn_out: bfloat16 [2, 768, 768], P('section', 'grp'), may hold values from -0.875 to 0.875
- mlp_in: bfloat16 [2, 768, 3072], P('section', 'grp'), may hold values from -0.21875 to 0.21875
- mlp_out: bfloat16 [2, 3072, 768], P('section', 'grp'), may hold values from -0.109375 to 0.109375
- norm_gains: float32 [2, 2, 768], P('section'), may hold values from 0.5 to 1.5
- cotangent: bfloat16 [32, 256, 768], P(('grp', 'dp')), may hold values from -6 to 6
Outputs:
- activations: bfloat16 [2, 32, 256, 768], P('section', ('grp', 'dp'))
- input_grads: float32 [2, 32, 256, 768], P('section', ('grp', 'dp'))
- grad_qkv: float32 [2, 768, 2304], P('section', 'grp')
- grad_attn_out: float32 [2, 768, 768], P('section', 'grp')
- grad_mlp_in: float32 [2, 768, 3072], P('section', 'grp')
- grad_mlp_out: float32 [2, 3072, 768], P('section', 'grp')
- grad_gains: float32 [2, 2, 768], P('section', None, 'grp')
- grad_table: float32 [1000, 768], P(('section', 'grp'))
- grad_mask_vector: float32 [768], P(('section', 'grp'))
Inputs may be any that keep to these rules, and one draw needn't show every extreme that they name: per-sequence timesteps, concentrated toward the high end; both ends are taken.
All inputs are finite; a program needn't handle non-finite values. No bound on the sum of `mask_flags` on one device may be relied on, other than what follows from the above.
Results may differ from a plain program's by a relative error of at most 0.018.
Values may be sent and summed in bfloat16 or wider, within the bound.
A program may use at most 192 MiB of HBM per device.

v0:
```python
import math

import jax
import jax.numpy as jnp
from jax import lax
from jax.sharding import PartitionSpec as P

HEADS = 12
HEAD = 64


def from_behind(value, axis, by):
    devices = lax.axis_size(axis)
    pairs = [(i, i + by) for i in range(devices) if 0 <= i + by < devices]
    return lax.ppermute(value, axis, pairs)


def layer_norm(hidden, gain_row):
    center = hidden - jnp.mean(hidden, axis=-1, keepdims=True)
    spread = jnp.mean(center * center, axis=-1, keepdims=True)
    return center * lax.rsqrt(spread + 1e-05) * gain_row


def gelu_tanh(upward_in):
    return jax.nn.gelu(upward_in, approximate=True)


def contract_rows(left, right):
    return lax.dot_general(
        left, right, (((0,), (0,)), ((), ())), preferred_element_type=jnp.float32
    )


def times_transpose(left, right):
    return lax.dot_general(
        left, right, (((1,), (1,)), ((), ())), preferred_element_type=jnp.float32
    )


def layer_forward(hidden, weights, gains):
    w_qkv, w_proj, w_up, w_down = weights
    length, model_width = hidden.shape
    scaling = 1.0 / math.sqrt(HEAD)
    normed = layer_norm(hidden, gains[0]).astype(jnp.bfloat16)
    packed = jnp.dot(normed, w_qkv, preferred_element_type=jnp.float32).astype(jnp.bfloat16)
    queries = packed[:, :model_width].reshape(length, HEADS, HEAD)
    attn_keys = packed[:, model_width : 2 * model_width].reshape(length, HEADS, HEAD)
    values = packed[:, 2 * model_width :].reshape(length, HEADS, HEAD)
    scores = (
        jnp.einsum("qhe,khe->hqk", queries, attn_keys, preferred_element_type=jnp.float32) * scaling
    )
    row_max = jnp.max(scores, axis=-1, keepdims=True)
    exp_scores = jnp.exp(scores - row_max)
    attn_probs = exp_scores / jnp.sum(exp_scores, axis=-1, keepdims=True)
    probs_low = attn_probs.astype(jnp.bfloat16)
    attn_mixed = (
        jnp.einsum("hqk,khe->qhe", probs_low, values, preferred_element_type=jnp.float32)
        .reshape(length, model_width)
        .astype(jnp.bfloat16)
    )
    middle = hidden + jnp.dot(attn_mixed, w_proj, preferred_element_type=jnp.float32)
    normed_two = layer_norm(middle, gains[1]).astype(jnp.bfloat16)
    upward = jnp.dot(normed_two, w_up, preferred_element_type=jnp.float32)
    activated = gelu_tanh(upward).astype(jnp.bfloat16)
    result = middle + jnp.dot(activated, w_down, preferred_element_type=jnp.float32)
    return (
        result,
        (
            normed,
            queries,
            attn_keys,
            values,
            attn_probs,
            probs_low,
            attn_mixed,
            middle,
            normed_two,
            upward,
            activated,
        ),
    )


def layer_backward(hidden, weights, gains, grad_out):
    w_qkv, w_proj, w_up, w_down = weights
    length, model_width = hidden.shape
    scaling = 1.0 / math.sqrt(HEAD)
    result, saved = layer_forward(hidden, weights, gains)
    (
        normed,
        queries,
        attn_keys,
        values,
        attn_probs,
        probs_low,
        attn_mixed,
        middle,
        normed_two,
        upward,
        activated,
    ) = saved
    grad_low = grad_out.astype(jnp.bfloat16)
    grad_down = contract_rows(activated, grad_low)
    grad_act = times_transpose(grad_low, w_down)
    upward_val, gelu_back = jax.vjp(gelu_tanh, upward)
    grad_upward = gelu_back(grad_act)[0].astype(jnp.bfloat16)
    grad_up = contract_rows(normed_two, grad_upward)
    grad_normed_two = times_transpose(grad_upward, w_up)
    norm_val, norm_back_two = jax.vjp(layer_norm, middle, gains[1])
    grad_mid_norm, gain_two = norm_back_two(grad_normed_two)
    grad_middle = grad_out + grad_mid_norm
    middle_low = grad_middle.astype(jnp.bfloat16)
    grad_proj = contract_rows(attn_mixed, middle_low)
    grad_mixed = (
        times_transpose(middle_low, w_proj).astype(jnp.bfloat16).reshape(length, HEADS, HEAD)
    )
    grad_probs = jnp.einsum("qhe,khe->hqk", grad_mixed, values, preferred_element_type=jnp.float32)
    grad_values = jnp.einsum(
        "hqk,qhe->khe", probs_low, grad_mixed, preferred_element_type=jnp.float32
    )
    row_inner = jnp.sum(grad_probs * attn_probs, axis=-1, keepdims=True)
    grad_scores = (attn_probs * (grad_probs - row_inner)).astype(jnp.bfloat16)
    grad_queries = (
        jnp.einsum("hqk,khe->qhe", grad_scores, attn_keys, preferred_element_type=jnp.float32)
        * scaling
    )
    grad_keys = (
        jnp.einsum("hqk,qhe->khe", grad_scores, queries, preferred_element_type=jnp.float32)
        * scaling
    )
    grad_packed = jnp.concatenate(
        [
            grad_queries.reshape(length, model_width),
            grad_keys.reshape(length, model_width),
            grad_values.reshape(length, model_width),
        ],
        axis=1,
    ).astype(jnp.bfloat16)
    grad_qkv = contract_rows(normed, grad_packed)
    grad_normed = times_transpose(grad_packed, w_qkv)
    norm_val_one, norm_back_one = jax.vjp(layer_norm, hidden, gains[0])
    grad_hid_norm, gain_one = norm_back_one(grad_normed)
    grad_input = grad_middle + grad_hid_norm
    return (grad_input, (grad_qkv, grad_proj, grad_up, grad_down), jnp.stack([gain_one, gain_two]))


def on_device(
    embeddings,
    mask_flags,
    timesteps,
    time_table,
    mask_vector,
    attn_qkv,
    attn_out,
    mlp_in,
    mlp_out,
    norm_gains,
    cotangent,
):
    micro_count = embeddings.shape[0]
    table_rows_count = time_table.shape[0]
    section_index = lax.axis_index("section")
    is_first = section_index == 0
    first_flag = is_first.astype(jnp.float32)
    gains_local = norm_gains[0]
    gathered = (
        lax.all_gather(attn_qkv[0], "grp", axis=0, tiled=True),
        lax.all_gather(attn_out[0], "grp", axis=0, tiled=True),
        lax.all_gather(mlp_in[0], "grp", axis=0, tiled=True),
        lax.all_gather(mlp_out[0], "grp", axis=0, tiled=True),
    )
    onehot = (timesteps[:, None] == jnp.arange(table_rows_count, dtype=jnp.int32)[None, :]).astype(
        jnp.bfloat16
    )
    table_rows = jnp.dot(onehot, time_table, preferred_element_type=jnp.float32)
    masked = mask_flags[..., None] == 1
    start_rows = (
        jnp.where(
            masked, mask_vector.astype(jnp.float32)[None, None, :], embeddings.astype(jnp.float32)
        )
        + table_rows[:, None, :]
    )
    received = jnp.zeros(embeddings.shape[1:], jnp.bfloat16)
    kept_inputs = []
    tick_outputs = []
    for tick_index in range(micro_count + 1):
        pick_index = min(tick_index, micro_count - 1)
        layer_input = jnp.where(is_first, start_rows[pick_index], received.astype(jnp.float32))
        kept_inputs.append(layer_input)
        result, saved = layer_forward(layer_input, gathered, gains_local)
        sent_rows = result.astype(jnp.bfloat16)
        tick_outputs.append(sent_rows)
        if tick_index < micro_count:
            received = from_behind(sent_rows, "section", 1)
    activations = jnp.stack(
        [
            jnp.where(is_first, tick_outputs[item], tick_outputs[item + 1])
            for item in range(micro_count)
        ]
    )[None]
    acc_terms = None
    recv_grad = jnp.zeros(embeddings.shape[1:], jnp.bfloat16)
    tick_grads = []
    for back_index in range(micro_count + 1):
        live_tick = jnp.where(is_first, back_index >= 1, back_index < micro_count)
        own_grad = cotangent[max(micro_count - 1 - back_index, 0)].astype(jnp.float32)
        grad_out = jnp.where(is_first, recv_grad.astype(jnp.float32), own_grad)
        grad_out = jnp.where(live_tick, grad_out, 0.0)
        grad_input, weight_terms, gain_terms = layer_backward(
            kept_inputs[micro_count - back_index], gathered, gains_local, grad_out
        )
        tick_grads.append(grad_input)
        new_terms = (weight_terms[0], weight_terms[1], weight_terms[2], weight_terms[3], gain_terms)
        if acc_terms is None:
            acc_terms = tuple(new_terms)
        else:
            acc_terms = tuple((total + part_term for total, part_term in zip(acc_terms, new_terms)))
        if back_index < micro_count:
            recv_grad = from_behind(grad_input.astype(jnp.bfloat16), "section", -1)
    shards = (
        lax.psum_scatter(
            acc_terms[0][None].astype(jnp.bfloat16), "grp", scatter_dimension=1, tiled=True
        ).astype(jnp.float32),
        lax.psum_scatter(
            acc_terms[1][None].astype(jnp.bfloat16), "grp", scatter_dimension=1, tiled=True
        ).astype(jnp.float32),
        lax.psum_scatter(
            acc_terms[2][None].astype(jnp.bfloat16), "grp", scatter_dimension=1, tiled=True
        ).astype(jnp.float32),
        lax.psum_scatter(
            acc_terms[3][None].astype(jnp.bfloat16), "grp", scatter_dimension=1, tiled=True
        ).astype(jnp.float32),
        lax.psum_scatter(
            acc_terms[4][None].astype(jnp.bfloat16), "grp", scatter_dimension=2, tiled=True
        ).astype(jnp.float32),
    )
    start_grads = jnp.stack([tick_grads[micro_count - item] for item in range(micro_count)])
    second_grads = jnp.stack([tick_grads[micro_count - 1 - item] for item in range(micro_count)])
    input_grads = jnp.where(is_first, jnp.where(masked, 0.0, start_grads), second_grads)[None]
    token_sums = jnp.sum(start_grads, axis=1)
    table_term = (
        jnp.dot(onehot.astype(jnp.float32).T, token_sums, precision=lax.Precision.HIGHEST)
        * first_flag
    )
    mask_term = jnp.sum(jnp.where(masked, start_grads, 0.0), axis=(0, 1)) * first_flag
    table_shards = (
        lax.psum_scatter(
            table_term.astype(jnp.bfloat16), ("section", "grp"), scatter_dimension=0, tiled=True
        ).astype(jnp.float32),
        lax.psum_scatter(
            mask_term.astype(jnp.bfloat16), ("section", "grp"), scatter_dimension=0, tiled=True
        ).astype(jnp.float32),
    )
    summed = (
        lax.psum(shards[0].astype(jnp.bfloat16), "dp").astype(jnp.float32),
        lax.psum(shards[1].astype(jnp.bfloat16), "dp").astype(jnp.float32),
        lax.psum(shards[2].astype(jnp.bfloat16), "dp").astype(jnp.float32),
        lax.psum(shards[3].astype(jnp.bfloat16), "dp").astype(jnp.float32),
        lax.psum(shards[4].astype(jnp.bfloat16), "dp").astype(jnp.float32),
        lax.psum(table_shards[0].astype(jnp.bfloat16), "dp").astype(jnp.float32),
        lax.psum(table_shards[1].astype(jnp.bfloat16), "dp").astype(jnp.float32),
    )
    return (
        activations,
        input_grads,
        summed[0],
        summed[1],
        summed[2],
        summed[3],
        summed[4],
        summed[5],
        summed[6],
    )


def solution(mesh):
    placed = (
        P(("grp", "dp"), None, None),
        P(("grp", "dp"), None),
        P(("grp", "dp")),
        P(),
        P(),
        P("section", "grp", None),
        P("section", "grp", None),
        P("section", "grp", None),
        P("section", "grp", None),
        P("section", None, None),
        P(("grp", "dp"), None, None),
    )
    return jax.shard_map(
        on_device,
        mesh=mesh,
        in_specs=placed,
        out_specs=(
            P("section", ("grp", "dp"), None, None),
            P("section", ("grp", "dp"), None, None),
            P("section", "grp", None),
            P("section", "grp", None),
            P("section", "grp", None),
            P("section", "grp", None),
            P("section", None, "grp"),
            P(("section", "grp"), None),
            P(("section", "grp")),
        ),
        check_vma=False,
    )
```

profile of v0, /device:TPU:0, one launch (start us, length us, event | category | flops | bytes accessed | tf_op | source)
XLA Modules:
  0.0 650.3 jit_solution(10015093173913044283)
XLA Ops:
  12.3 30.8 %all-gather.9.cloned.1.call-done = bf16[1,768,2304]{2,1,0:T(8,128)(2,1)} async-done(((bf16[1,192,2304]{2,1,0:T(8,128)(2,1)}), bf16[1,768,2304]{2,1,0:T(8,128)(2,1)}) %all-gather.9.cloned.1.call-update) | async-done | bytes 3538960 | tf_op jit(solution)/shard_map/all_gather | solution.py:167
  43.1 3.2 convolution_convert_fusion.2
  46.9 2.9 fusion.191
  49.9 2.4 convolution_convert_fusion.11
  52.3 9.8 %all-gather.11.cloned.1.call-done = bf16[1,768,768]{2,1,0:T(8,128)(2,1)} async-done(((bf16[1,192,768]{2,1,0:T(8,128)(2,1)}), bf16[1,768,768]{2,1,0:T(8,128)(2,1)}) %all-gather.11.cloned.1.call-update) | async-done | bytes 1179664 | tf_op jit(solution)/shard_map/all_gather | solution.py:168
  64.2 36.9 %all-gather.13.cloned.1.call-done = bf16[1,768,3072]{2,1,0:T(8,128)(2,1)} async-done(((bf16[1,192,3072]{2,1,0:T(8,128)(2,1)}), bf16[1,768,3072]{2,1,0:T(8,128)(2,1)}) %all-gather.13.cloned.1.call-update) | async-done | bytes 4718608 | tf_op jit(solution)/shard_map/all_gather | solution.py:169
  101.2 5.5 fusion.26
  106.7 33.4 %all-gather.15.cloned.1.call-done = bf16[1,3072,768]{2,1,0:T(8,128)(2,1)} async-done(((bf16[1,768,768]{2,1,0:T(8,128)(2,1)}), bf16[1,3072,768]{2,1,0:T(8,128)(2,1)}) %all-gather.15.cloned.1.call-update) | async-done | bytes 4718608 | tf_op jit(solution)/shard_map/all_gather | solution.py:170
  140.0 5.4 fusion.97
  145.4 3.6 collective-permute-start
  149.1 8.5 %collective-permute-done = bf16[256,768]{1,0:T(8,128)(2,1)S(1)} collective-permute-done((bf16[256,768]{1,0:T(8,128)(2,1)S(1)}, bf16[256,768]{1,0:T(8,128)(2,1)S(1)}, u32[]{:S(2)}, u32[]{:S(2)}) %collective-permute-start) | collective-permute-done | bytes 393248 | tf_op jit(solution)/shard_map/ppermute | solution.py:15
  162.3 2.9 fusion.193
  165.3 2.4 convolution_convert_fusion.10
  168.6 4.2 fusion.24
  174.9 5.2 collective-permute-start.1
  180.0 7.1 %collective-permute-done.1 = bf16[256,768]{1,0:T(8,128)(2,1)} collective-permute-done((bf16[256,768]{1,0:T(8,128)(2,1)S(1)}, bf16[256,768]{1,0:T(8,128)(2,1)}, u32[]{:S(2)}, u32[]{:S(2)}) %collective-permute-start.1) | collective-permute-done | bytes 393248 | tf_op jit(solution)/shard_map/ppermute | solution.py:15
  188.6 3.2 convolution_convert_fusion
  194.8 2.1 copy.90
  196.9 3.9 fusion.195
  200.8 2.5 convolution_convert_fusion.9
  204.2 4.6 fusion.22
  208.9 3.4 fusion.60
  218.4 2.8 convolution_convert_fusion.7
  231.5 4.1 fusion.128
  235.6 6.2 collective-permute-done.2
  241.8 3.1 fusion.53
  249.5 2.8 convolution_convert_fusion.5
  261.0 4.2 fusion.127
  265.2 5.3 collective-permute-done.3
  270.5 4.1 fusion.46
  280.6 4.6 multiply_reduce_fusion
  286.9 3.4 multiply_convert_fusion
  295.3 6.5 %fusion.30 = bf16[1,768,2304]{2,1,0:T(8,128)(2,1)} fusion(f32[768,2304]{1,0:T(8,128)S(1)} %bitcast.271, f32[768,2304]{1,0:T(8,128)} %fusion.127, bf16[256,768]{0,1:T(8,128)(2,1)S(1)} %bitcast.322, bf16[256,768]{0,1:T(8,128)(2,1)S(1)} %bitcast.301, bf16[256,768]{0,1:T(8,128)(2,1)S(1)} %bitcast.303, f32[768]{0:T(1024)S(1)} %get-tuple-element.24, ...), kind=kOutput, calls=%fused_computation.38 | convolution fusion | flops 915800064 | bytes 19666944 | tf_op jit(solution)/shard_map/dot_general | solution.py:29
  306.7 5.4 fusion.28
  313.2 4.3 fusion.136
  317.6 6.5 %fusion.145 = f32[3072,768]{1,0:T(8,128)} fusion(bf16[256,768]{1,0:T(8,128)(2,1)S(1)} %copy-done.68, pred[]{:T(512)S(6)} %eq.23, bf16[2,256,768]{2,1,0:T(8,128)(2,1)S(1)} %copy-done.28, f32[256,3072]{1,0:T(8,128)S(1)} %copy-done.38), kind=kOutput, calls=%fused_computation.218 | convolution fusion | flops 1215823872 | bytes 13369345 | tf_op jit(solution)/shard_map/dot_general | solution.py:29
  324.1 6.6 %fusion.29 = bf16[1,3072,768]{2,1,0:T(8,128)(2,1)} fusion(f32[3072,768]{1,0:T(8,128)S(1)} %fusion.136, f32[3072,768]{1,0:T(8,128)} %fusion.145, bf16[256,768]{1,0:T(8,128)(2,1)S(1)} %copy-done.70, pred[]{:T(512)S(6)} %eq.23, bf16[2,256,768]{2,1,0:T(8,128)(2,1)S(1)} %copy-done.28, f32[256,3072]{1,0:T(8,128)S(1)} %copy-done.40), kind=kOutput, calls=%fused_computation.37 | convolution fusion | flops 1223098368 | bytes 27525120 | tf_op jit(solution)/shard_map/dot_general | solution.py:29
  332.7 3.4 multiply_reduce_fusion.7
  339.5 27.6 %fusion = bf16[128,768]{1,0:T(8,128)(2,1)S(1)} fusion(bf16[1000,768]{1,0:T(8,128)(2,1)S(1)} %multiply_convert_fusion.6), kind=kCustom, calls=%all-reduce-scatter | all-reduce-scatter fusion | flops 786433 | bytes 1733120
  367.1 4.1 collective-permute-start.4
  373.6 44.0 %reduce-scatter.14.cloned.1.call-done = bf16[1,192,3072]{2,1,0:T(8,128)(2,1)} async-done(((bf16[1,768,3072]{2,1,0:T(8,128)(2,1)}), bf16[1,192,3072]{2,1,0:T(8,128)(2,1)}) %reduce-scatter.14.cloned.1.call-update) | async-done | bytes 1179664 | tf_op jit(solution)/shard_map/reduce_scatter | solution.py:227
  417.6 50.5 %reduce-scatter.16.cloned.1.call-done = bf16[1,768,768]{2,1,0:T(8,128)(2,1)} async-done(((bf16[1,3072,768]{2,1,0:T(8,128)(2,1)}), bf16[1,768,768]{2,1,0:T(8,128)(2,1)}) %reduce-scatter.16.cloned.1.call-update) | async-done | bytes 1179664 | tf_op jit(solution)/shard_map/reduce_scatter | solution.py:230
  468.9 5.3 fusion.115
  475.2 12.5 %all-reduce.1 = bf16[768]{0:T(1024)(128)(2,1)S(1)} all-reduce(bf16[768]{0:T(1024)(128)(2,1)S(1)} %multiply_convert_fusion.13), channel_id=12, replica_groups=mesh['section'=2,'grp'=4,'dp'=4] {'section','grp'}, use_global_device_ids=true, to_apply=%region_53.54.clone | all-reduce | flops 768 | bytes 3072
  487.8 2.5 fusion.76
  491.9 11.8 %all-reduce.3 = (bf16[1,2,192]{2,1,0:T(2,128)(2,1)S(1)}, bf16[96]{0:T(256)(128)(2,1)S(1)}) all-reduce(bf16[1,2,192]{2,1,0:T(2,128)(2,1)S(1)} %copy.117, bf16[96]{0:T(256)(128)(2,1)S(1)} %dynamic-slice.3), channel_id=1, replica_groups=mesh['section'=2,'grp'=4,'dp'=4] {'dp'}, use_global_device_ids=true, to_apply=%region_48.49 | all-reduce | flops 480 | bytes 1920 | tf_op jit(solution)/shard_map/psum | solution.py:259
  504.8 129.6 %all-reduce.7.cloned.1.call-done = (bf16[1,192,2304]{2,1,0:T(8,128)(2,1)}, bf16[1,192,768]{2,1,0:T(8,128)(2,1)}, bf16[1,192,3072]{2,1,0:T(8,128)(2,1)}, bf16[1,768,768]{2,1,0:T(8,128)(2,1)}, bf16[125,768]{1,0:T(8,128)(2,1)}) async-done(((bf16[1,192,2304]{2,1,0:T(8,128)(2,1)}, bf16[1,192,768]{2,1,0:T(8,128)(2,1)}, bf16[1,192,3072]{2,1,0:T(8,128)(2,1)}, bf16[1,768,768]{2,1,0:T(8,128)(2,1)}, ...) | async-done | bytes 3730960 | tf_op jit(solution)/shard_map/psum | solution.py:255
  634.4 2.6 convert_element_type.321
  (390 shorter events, 84.5 us)
Async XLA Ops:
  7.2 35.9 %all-gather.9.cloned.1.call-start = ((), (), s32[]{:S(2)}) async-start(), calls=%async_computation.9 | async-start | bytes 4423680 | tf_op jit(solution)/shard_map/all_gather | solution.py:167
  8.0 54.2 %all-gather.11.cloned.1.call-start = ((), (), s32[]{:S(2)}) async-start(), calls=%async_computation.10 | async-start | bytes 1474560 | tf_op jit(solution)/shard_map/all_gather | solution.py:168
  8.7 92.4 %all-gather.13.cloned.1.call-start = ((), (), s32[]{:S(2)}) async-start(), calls=%async_computation.11 | async-start | bytes 5898240 | tf_op jit(solution)/shard_map/all_gather | solution.py:169
  9.5 130.6 %all-gather.15.cloned.1.call-start = ((), (), s32[]{:S(2)}) async-start(), calls=%async_computation.12 | async-start | bytes 5898240 | tf_op jit(solution)/shard_map/all_gather | solution.py:170
  10.0 363.6 %reduce-scatter.12.cloned.1.call-start = ((), (), s32[]{:S(2)}) async-start(), calls=%async_computation.6 | async-start | bytes 1474560 | tf_op jit(solution)/shard_map/reduce_scatter | solution.py:224
  10.2 36.1 %copy-start.89 = (pred[2,256]{1,0:T(4,128)(4,1)}, pred[2,256]{1,0:T(4,128)(4,1)S(1)}, u32[]{:S(2)}) copy-start(pred[2,256]{1,0:T(4,128)(4,1)S(1)} %broadcast_compare_fusion) | copy-start | bytes 1540
  11.9 281.2 %copy-start.3 = (f32[2,256,768]{2,1,0:T(8,128)}, f32[2,256,768]{2,1,0:T(8,128)S(1)}, u32[]{:S(2)}) copy-start(f32[2,256,768]{2,1,0:T(8,128)S(1)} %select_add_fusion) | copy-start | bytes 4718596
  12.3 34.1 %copy-start.91 = (f32[256]{0:T(256)}, f32[256]{0:T(256)S(1)}, u32[]{:S(2)}) copy-start(f32[256]{0:T(256)S(1)} %multiply_reduce_fusion.23) | copy-start | bytes 3076
  52.3 54.4 %copy-start.46 = (bf16[12,64,256]{2,1,0:T(8,128)(2,1)}, bf16[12,64,256]{2,1,0:T(8,128)(2,1)S(1)}, u32[]{:S(2)}) copy-start(bf16[12,64,256]{2,1,0:T(8,128)(2,1)S(1)} %convolution_convert_fusion.11) | copy-start | bytes 1179652
  64.0 76.1 %copy-start.11 = (f32[256,768]{1,0:T(8,128)}, f32[256,768]{1,0:T(8,128)S(1)}, u32[]{:S(2)}) copy-start(f32[256,768]{1,0:T(8,128)S(1)} %get-tuple-element.68) | copy-start | bytes 2359300
  140.0 18.0 %copy-start.99 = (bf16[1,768,2304]{2,1,0:T(8,128)(2,1)S(1)}, bf16[1,768,2304]{2,1,0:T(8,128)(2,1)}, u32[]{:S(2)}) copy-start(bf16[1,768,2304]{2,1,0:T(8,128)(2,1)} %all-gather.9.cloned.1.call-done) | copy-start | bytes 10616836
  145.4 12.6 %copy-start.82 = (bf16[256,768]{1,0:T(8,128)(2,1)}, bf16[256,768]{1,0:T(8,128)(2,1)S(1)}, u32[]{:S(2)}) copy-start(bf16[256,768]{1,0:T(8,128)(2,1)S(1)} %fusion.97) | copy-start | bytes 1179652
  145.4 12.1 %collective-permute-start = (bf16[256,768]{1,0:T(8,128)(2,1)S(1)}, bf16[256,768]{1,0:T(8,128)(2,1)S(1)}, u32[]{:S(2)}, u32[]{:S(2)}) collective-permute-start(bf16[256,768]{1,0:T(8,128)(2,1)S(1)} %fusion.97), channel_id=1, source_target_pairs={{0,16},{1,17},{2,18},{3,19},{4,20},{5,21},{6,22},{7,23},{8,24},{9,... | collective-permute-start | bytes 1179656 | tf_op jit(solution)/shard_map/ppermute | solution.py:15
  174.8 13.7 %copy-start.84 = (bf16[256,768]{1,0:T(8,128)(2,1)}, bf16[256,768]{1,0:T(8,128)(2,1)S(1)}, u32[]{:S(2)}) copy-start(bf16[256,768]{1,0:T(8,128)(2,1)S(1)} %fusion.94) | copy-start | bytes 1179652
  174.9 12.3 %collective-permute-start.1 = (bf16[256,768]{1,0:T(8,128)(2,1)S(1)}, bf16[256,768]{1,0:T(8,128)(2,1)}, u32[]{:S(2)}, u32[]{:S(2)}) collective-permute-start(bf16[256,768]{1,0:T(8,128)(2,1)S(1)} %fusion.94), channel_id=1, source_target_pairs={{0,16},{1,17},{2,18},{3,19},{4,20},{5,21},{6,22},{7,23},{8,24},{9,... | collective-permute-start | bytes 1179656 | tf_op jit(solution)/shard_map/ppermute | solution.py:15
  194.8 8.5 %copy-start.56 = (bf16[256,768]{0,1:T(8,128)(2,1)}, bf16[256,768]{0,1:T(8,128)(2,1)S(1)}, u32[]{:S(2)}) copy-start(bf16[256,768]{0,1:T(8,128)(2,1)S(1)} %copy.89) | copy-start | bytes 1179652
  203.9 10.0 %copy-start.19 = (f32[256,768]{1,0:T(8,128)}, f32[256,768]{1,0:T(8,128)S(1)}, u32[]{:S(2)}) copy-start(f32[256,768]{1,0:T(8,128)S(1)} %get-tuple-element.76) | copy-start | bytes 2359300
  204.2 8.1 %slice-start.10 = ((s8[4718592]{0:T(1024)(128)(4,1)}), s8[4194304]{0:T(1024)(128)(4,1)S(1)}, s32[]{:S(2)}) async-start(s8[4718592]{0:T(1024)(128)(4,1)} %bitcast.332), calls=%async_computation.25 | async-start | bytes 8388608
  227.0 14.8 %slice-start.6 = ((s8[4718592]{0:T(1024)(128)(4,1)}), s8[4194304]{0:T(1024)(128)(4,1)S(1)}, s32[]{:S(2)}) async-start(s8[4718592]{0:T(1024)(128)(4,1)} %bitcast.328), calls=%async_computation.21 | async-start | bytes 8388608
  228.7 13.1 %slice-start.7 = ((s8[4718592]{0:T(1024)(128)(4,1)}), s8[524288]{0:T(1024)(128)(4,1)S(1)}, s32[]{:S(2)}) async-start(s8[4718592]{0:T(1024)(128)(4,1)} %bitcast.328), calls=%async_computation.22 | async-start | bytes 1048576
  229.9 11.9 %copy-start.37 = (f32[256,3072]{1,0:T(8,128)S(1)}, f32[256,3072]{1,0:T(8,128)}, u32[]{:S(2)}) copy-start(f32[256,3072]{1,0:T(8,128)} %copy-done.36) | copy-start | bytes 9437188
  229.9 11.9 %collective-permute-start.2 = (bf16[256,768]{1,0:T(8,128)(2,1)S(1)}, bf16[256,768]{1,0:T(8,128)(2,1)S(1)}, u32[]{:S(2)}, u32[]{:S(2)}) collective-permute-start(bf16[256,768]{1,0:T(8,128)(2,1)S(1)} %get-tuple-element.51), channel_id=1, source_target_pairs={{16,0},{17,1},{18,2},{19,3},{20,4},{21,5},{22,6},{23,7},{24,8},{25... | collective-permute-start | bytes 1179656 | tf_op jit(solution)/shard_map/ppermute | solution.py:15
  231.4 13.5 %slice-start.12 = ((s8[4718592]{0:T(1024)(128)(4,1)}), s8[4194304]{0:T(1024)(128)(4,1)S(1)}, s32[]{:S(2)}) async-start(s8[4718592]{0:T(1024)(128)(4,1)} %bitcast.334), calls=%async_computation.27 | async-start | bytes 8388608
  235.6 9.4 %copy-start.23 = (f32[256,768]{1,0:T(8,128)S(1)}, f32[256,768]{1,0:T(8,128)}, u32[]{:S(2)}) copy-start(f32[256,768]{1,0:T(8,128)} %copy-done.22) | copy-start | bytes 2359300
  235.6 9.4 %slice-start.13 = ((s8[4718592]{0:T(1024)(128)(4,1)}), s8[524288]{0:T(1024)(128)(4,1)S(1)}, s32[]{:S(2)}) async-start(s8[4718592]{0:T(1024)(128)(4,1)} %bitcast.334), calls=%async_computation.28 | async-start | bytes 1048576
  256.6 13.9 %slice-start.8 = ((s8[4718592]{0:T(1024)(128)(4,1)}), s8[4194304]{0:T(1024)(128)(4,1)S(1)}, s32[]{:S(2)}) async-start(s8[4718592]{0:T(1024)(128)(4,1)} %bitcast.330), calls=%async_computation.23 | async-start | bytes 8388608
  258.3 12.2 %slice-start.9 = ((s8[4718592]{0:T(1024)(128)(4,1)}), s8[524288]{0:T(1024)(128)(4,1)S(1)}, s32[]{:S(2)}) async-start(s8[4718592]{0:T(1024)(128)(4,1)} %bitcast.330), calls=%async_computation.24 | async-start | bytes 1048576
  259.4 11.1 %copy-start.27 = (bf16[2,256,768]{2,1,0:T(8,128)(2,1)S(1)}, bf16[2,256,768]{2,1,0:T(8,128)(2,1)}, u32[]{:S(2)}) copy-start(bf16[2,256,768]{2,1,0:T(8,128)(2,1)} %param.21) | copy-start | bytes 2359300
  259.4 11.1 %copy-start.39 = (f32[256,3072]{1,0:T(8,128)S(1)}, f32[256,3072]{1,0:T(8,128)}, u32[]{:S(2)}) copy-start(f32[256,3072]{1,0:T(8,128)} %fusion.26) | copy-start | bytes 9437188
  259.4 11.1 %collective-permute-start.3 = (bf16[256,768]{1,0:T(8,128)(2,1)S(1)}, bf16[256,768]{1,0:T(8,128)(2,1)S(1)}, u32[]{:S(2)}, u32[]{:S(2)}) collective-permute-start(bf16[256,768]{1,0:T(8,128)(2,1)S(1)} %get-tuple-element.36), channel_id=1, source_target_pairs={{16,0},{17,1},{18,2},{19,3},{20,4},{21,5},{22,6},{23,7},{24,8},{25... | collective-permute-start | bytes 1179656 | tf_op jit(solution)/shard_map/ppermute | solution.py:15
  261.0 13.7 %slice-start.14 = ((s8[4718592]{0:T(1024)(128)(4,1)}), s8[4194304]{0:T(1024)(128)(4,1)S(1)}, s32[]{:S(2)}) async-start(s8[4718592]{0:T(1024)(128)(4,1)} %bitcast.336), calls=%async_computation.29 | async-start | bytes 8388608
  265.2 9.4 %copy-start.12 = (f32[256,768]{1,0:T(8,128)S(1)}, f32[256,768]{1,0:T(8,128)}, u32[]{:S(2)}) copy-start(f32[256,768]{1,0:T(8,128)} %copy-done.11) | copy-start | bytes 2359300
  265.2 9.4 %slice-start.15 = ((s8[4718592]{0:T(1024)(128)(4,1)}), s8[524288]{0:T(1024)(128)(4,1)S(1)}, s32[]{:S(2)}) async-start(s8[4718592]{0:T(1024)(128)(4,1)} %bitcast.336), calls=%async_computation.30 | async-start | bytes 1048576
  270.5 6.1 copy-start.69
  286.8 86.8 %reduce-scatter.10.cloned.1.call-start = ((), (), s32[]{:S(2)}) async-start(), calls=%async_computation.5 | async-start | bytes 4423680 | tf_op jit(solution)/shard_map/reduce_scatter | solution.py:221
  301.8 115.8 %reduce-scatter.14.cloned.1.call-start = ((), (), s32[]{:S(2)}) async-start(), calls=%async_computation.7 | async-start | bytes 5898240 | tf_op jit(solution)/shard_map/reduce_scatter | solution.py:227
  312.1 156.0 %reduce-scatter.16.cloned.1.call-start = ((), (), s32[]{:S(2)}) async-start(), calls=%async_computation.8 | async-start | bytes 5898240 | tf_op jit(solution)/shard_map/reduce_scatter | solution.py:230
  317.6 6.5 %copy-start.40 = (f32[256,3072]{1,0:T(8,128)S(1)}, f32[256,3072]{1,0:T(8,128)}, u32[]{:S(2)}) copy-start(f32[256,3072]{1,0:T(8,128)} %fusion.26) | copy-start | bytes 9437188
  317.6 6.5 %copy-start.70 = (bf16[256,768]{1,0:T(8,128)(2,1)S(1)}, bf16[256,768]{1,0:T(8,128)(2,1)}, u32[]{:S(2)}) copy-start(bf16[256,768]{1,0:T(8,128)(2,1)} %copy-done.69) | copy-start | bytes 1179652
  330.8 160.2 %reduce-scatter.18.cloned.1.call-start = ((), (), s32[]{:S(2)}) async-start(), calls=%async_computation.13 | async-start | bytes 245760
  367.0 101.8 %copy-start.83 = (bf16[256,768]{1,0:T(8,128)(2,1)S(1)}, bf16[256,768]{1,0:T(8,128)(2,1)}, u32[]{:S(2)}) copy-start(bf16[256,768]{1,0:T(8,128)(2,1)} %copy-done.82) | copy-start | bytes 1179652
  367.1 101.8 %copy-start.85 = (bf16[256,768]{1,0:T(8,128)(2,1)S(1)}, bf16[256,768]{1,0:T(8,128)(2,1)}, u32[]{:S(2)}) copy-start(bf16[256,768]{1,0:T(8,128)(2,1)} %copy-done.84) | copy-start | bytes 1179652
  367.1 5.4 collective-permute-start.4
  372.4 96.5 %copy-start.21 = (f32[256,768]{1,0:T(8,128)S(1)}, f32[256,768]{1,0:T(8,128)}, u32[]{:S(2)}) copy-start(f32[256,768]{1,0:T(8,128)} %copy-done.19) | copy-start | bytes 2359300
  372.4 262.0 %all-reduce.7.cloned.1.call-start = ((), (), s32[]{:S(2)}) async-start(), calls=%async_computation.14 | async-start | bytes 7471104 | tf_op jit(solution)/shard_map/psum | solution.py:255
  468.9 18.9 %copy-start.32 = (f32[256,768]{1,0:T(8,128)S(1)}, f32[256,768]{1,0:T(8,128)}, u32[]{:S(2)}) copy-start(f32[256,768]{1,0:T(8,128)} %get-tuple-element.37) | copy-start | bytes 2359300
  468.9 18.9 %copy-start.44 = (f32[1,1,256,768]{3,2,1,0:T(8,128)S(1)}, f32[1,1,256,768]{3,2,1,0:T(8,128)}, u32[]{:S(2)}) copy-start(f32[1,1,256,768]{3,2,1,0:T(8,128)} %get-tuple-element.50) | copy-start | bytes 2359300
  634.4 6.1 copy-start.73
  (85 other events, 231.5 us)
Sparse Core Ops, SparseCore 0:
  9.6 33.4 all-gather.8
  44.7 17.4 all-gather.10
  63.7 37.4 all-gather.12
  102.6 37.4 all-gather.14
  286.9 24.7 reduce-scatter.11
  314.1 52.2 reduce-scatter.9
  368.9 48.6 reduce-scatter.13
  420.1 47.9 reduce-scatter.15
  471.2 19.7 reduce-scatter.17
  494.2 140.2 all-reduce.6
where the time goes:
time: 657 us; the launch traced here: 650 us
  waiting for transfers between devices  366 us (56%)
  matrix products  141 us (21%)
  blocking collectives  51.9 us (8%)
  local copies, waits for them, and re-layouts  28.4 us (4%)
  other arithmetic  28.3 us (4%)
  between operations  17.8 us (3%)
  starting transfers between devices  16.9 us (3%)
    psum x1, waiting for transfers between devices, on_device(): lax.psum(shards[0].astype(jnp.bfloat16), 'dp').astype(jnp.float32)  130 us
    reduce_scatter x1, waiting for transfers between devices, on_device(): lax.psum_scatter(acc_terms[3][None].astype(jnp.bfloat16), 'grp', scatter_...  50.5 us
    dot_general x12, matrix products, contract_rows(): lax.dot_general(left, right, (((0,), (0,)), ((), ())), preferred_element_...  46.1 us
    reduce_scatter x1, waiting for transfers between devices, on_device(): lax.psum_scatter(acc_terms[2][None].astype(jnp.bfloat16), 'grp', scatter_...  44 us
    unnamed x2, blocking collectives  40.1 us
    all_gather x1, waiting for transfers between devices, on_device(): lax.all_gather(mlp_in[0], 'grp', axis=0, tiled=True)  36.9 us
    all_gather x1, waiting for transfers between devices, on_device(): lax.all_gather(mlp_out[0], 'grp', axis=0, tiled=True)  33.4 us
    all_gather x1, waiting for transfers between devices, on_device(): lax.all_gather(attn_qkv[0], 'grp', axis=0, tiled=True)  30.8 us
  transfers between devices with their start and end apart: 15, of which 12 were waited for; matrix products, arithmetic and copies ran while one was open for 17% of the time, Pallas kernels for 0%

commit v1 on v0

v1 whole, which is shorter than its diff:
```python
import functools
import math

import jax
import jax.numpy as jnp
from jax import lax
from jax.experimental import pallas as pl
from jax.experimental.pallas import tpu as pltpu
from jax.sharding import PartitionSpec as P

HEADS = 12
HEAD = 64
BF = jnp.bfloat16
F32 = jnp.float32
MESH = pl.DeviceIdType.MESH
EPS = 1e-05
GELU_C = math.sqrt(2.0 / math.pi)

OUT0, IN0, PROJ, QKV0, CHUNKS = 0, 4, 8, 9, 12
GATHER_ORDER = (9, 10, 11, 8, 4, 5, 6, 7, 0, 1, 2, 3)


def dot_nn(a, b):
    return lax.dot_general(a, b, (((1,), (0,)), ((), ())), preferred_element_type=F32)


def dot_nt(a, b):
    return lax.dot_general(a, b, (((1,), (1,)), ((), ())), preferred_element_type=F32)


def dot_tn(a, b):
    return lax.dot_general(a, b, (((0,), (0,)), ((), ())), preferred_element_type=F32)


def loop(n, body):
    lax.fori_loop(0, n, lambda i, c: (body(i), c)[1], 0)


def mega(
    cfg,
    times_ref,
    mask_ref,
    vector_ref,
    gains_ref,
    emb_hbm,
    cot_hbm,
    table_hbm,
    wq_hbm,
    wp_hbm,
    wi_hbm,
    wo_hbm,
    act_out,
    dx_out,
    grad_out,
    small_out,
    table_out,
    w,
    h,
    mid,
    acc,
    tmp,
    normed,
    mixed,
    n2,
    actv,
    gp,
    packed,
    probs,
    glow,
    dmlow,
    dpk,
    do_ref,
    outb,
    relay,
    maskc,
    trow,
    pay,
    gains_acc,
    cbuf,
    ybuf,
    z1,
    z2,
    in_sem,
    own_sem,
    gsend,
    grecv,
    rsend,
    rrecv,
    csend,
    crecv,
    usend,
    urecv,
    psend,
    precv,
    osem,
    *extra,
):
    count, seq, width, nz, unit = cfg
    quarter = width // 4
    units = CHUNKS * quarter // unit
    per_block = quarter // unit
    table_rows = table_hbm.shape[0]
    s = lax.axis_index("section")
    g = lax.axis_index("grp")
    d = lax.axis_index("dp")
    x0 = s == 0
    x1 = jnp.logical_not(x0)
    c = lax.rem(g, 2)
    y = g // 2
    twin = g + 1 - 2 * c
    across = lax.rem(g + 2, 4)
    zpair = d + 1 - 2 * lax.rem(d, 2)
    zfar = lax.rem(d + 2, 4)
    half = lax.rem(d, 2)

    peers = [{"section": 1 - s}, {"grp": twin}, {"grp": across}, {"dp": zpair}]
    if nz == 4:
        peers += [{"dp": 3 - d}, {"dp": zfar}]
    barrier = pltpu.get_barrier_semaphore()
    for peer in peers:
        pl.semaphore_signal(barrier, inc=1, device_id=peer, device_id_type=MESH)
    pl.semaphore_wait(barrier, len(peers))

    def remote(src, dst, send, recv, peer):
        return pltpu.make_async_remote_copy(
            src_ref=src, dst_ref=dst, send_sem=send, recv_sem=recv, device_id=peer, device_id_type=MESH
        )

    def rows(start, size, by):
        return pl.ds(pl.multiple_of(start, by), size)

    def place(i, q):
        return jnp.where(i < IN0, q * width + quarter * i, i * width + quarter * q)

    def source(i):
        if i < IN0:
            return wo_hbm.at[pl.ds(i * quarter, quarter)]
        if i < PROJ:
            return wi_hbm.at[:, pl.ds((i - IN0) * width, width)]
        if i == PROJ:
            return wp_hbm
        return wq_hbm.at[:, pl.ds((i - QKV0) * width, width)]

    hq = quarter // 2
    far = across
    far_twin = lax.rem(twin + 2, 4)

    def own_copy(i):
        return pltpu.make_async_copy(source(i), w.at[rows(place(i, g), quarter, hq)], own_sem.at[i])

    def own_to_twin(i):
        return remote(source(i), w.at[rows(place(i, g), quarter, hq)], gsend.at[0, i], grecv.at[0, i], {"grp": twin})

    def own_across(i):
        return remote(
            source(i).at[rows(half * hq, hq, hq)],
            w.at[rows(place(i, g) + half * hq, hq, hq)],
            gsend.at[1, i],
            grecv.at[1, i],
            {"grp": across},
        )

    def y_half(i, q):
        return w.at[rows(place(i, q) + half * hq, hq, hq)]

    def z_half(i, q):
        return w.at[rows(place(i, q) + (1 - half) * hq, hq, hq)]

    def y_to_z(i):
        return remote(y_half(i, far), y_half(i, far), gsend.at[2, i], grecv.at[2, i], {"dp": zpair})

    def y_to_twin(i):
        return remote(y_half(i, far), y_half(i, far), gsend.at[3, i], grecv.at[3, i], {"grp": twin})

    def z_to_twin(i):
        return remote(z_half(i, far), z_half(i, far), gsend.at[4, i], grecv.at[4, i], {"grp": twin})

    def recv_y(i):
        remote(y_half(i, far), y_half(i, far), gsend.at[1, i], grecv.at[1, i], {"grp": across}).wait_recv()

    def recv_z(i):
        remote(z_half(i, far), z_half(i, far), gsend.at[2, i], grecv.at[2, i], {"dp": zpair}).wait_recv()

    def near_ready(i):
        dst = w.at[rows(place(i, twin), quarter, hq)]
        remote(dst, dst, gsend.at[0, i], grecv.at[0, i], {"grp": twin}).wait_recv()
        own_copy(i).wait()

    def far_ready(i):
        dst = y_half(i, far_twin)
        remote(dst, dst, gsend.at[3, i], grecv.at[3, i], {"grp": twin}).wait_recv()
        dst = z_half(i, far_twin)
        remote(dst, dst, gsend.at[4, i], grecv.at[4, i], {"grp": twin}).wait_recv()

    def gather_order(k):
        return jnp.where(k < 3, QKV0 + k, jnp.where(k == 3, PROJ, jnp.where(k < 8, k, k - 8)))

    zlag = 2
    gather_steps = CHUNKS + zlag

    def gather_step(k):
        @pl.when(k < CHUNKS)
        def _():
            i = gather_order(k)
            recv_y(i)
            y_to_z(i).start()
            y_to_twin(i).start()

        @pl.when(k >= zlag)
        def _():
            i = gather_order(k - zlag)
            recv_z(i)
            z_to_twin(i).start()

    def load(src, dst, k):
        return pltpu.make_async_copy(src, dst, in_sem.at[k])

    table_copy = load(table_hbm, dpk.at[pl.ds(0, table_rows)], 0)
    emb_copy = load(emb_hbm, outb, 1)

    def cot_copy(mb):
        return load(cot_hbm.at[mb], glow.at[rows(mb * seq, seq, seq)], 2 + mb)

    for i in GATHER_ORDER:
        own_across(i).start()
    for i in GATHER_ORDER:
        own_to_twin(i).start()
        own_copy(i).start()

    @pl.when(x0)
    def _():
        table_copy.start()
        emb_copy.start()

    @pl.when(x1)
    def _():
        for mb in range(2):
            cot_copy(mb).start()

    def chunk(k):
        return w[rows(k * width, width, width), :]

    step_rows = 64
    parts_of = seq // step_rows
    lane = lax.broadcasted_iota(jnp.int32, (1, 128), 1)
    low_half = (lane < HEAD).astype(F32)
    masks = (low_half.astype(BF), (1.0 - low_half).astype(BF))
    scaled = ((low_half * 0.125).astype(BF), ((1.0 - low_half) * 0.125).astype(BF))

    def seq_rows(mb):
        return rows(mb * seq, seq, seq)

    def sub_rows(mb, r):
        return rows(mb * seq + r * step_rows, step_rows, step_rows)

    def r_rows(r):
        return rows(r * step_rows, step_rows, step_rows)

    def norm_parts(v):
        center = v - jnp.mean(v, axis=-1, keepdims=True)
        spread = jnp.mean(center * center, axis=-1, keepdims=True)
        inv = lax.rsqrt(spread + EPS)
        return center * inv, inv

    pay[...] = jnp.zeros_like(pay)
    gains_acc[...] = jnp.zeros_like(gains_acc)
    for mb in range(2):
        maskc[mb] = jnp.transpose(jnp.broadcast_to(mask_ref[mb : mb + 1, :].astype(F32), (128, seq)))

    @pl.when(x0)
    def _():
        table_copy.wait()
        emb_copy.wait()
        ids = lax.broadcasted_iota(jnp.int32, (8, table_rows), 1)
        pick = lax.broadcasted_iota(jnp.int32, (8, table_rows), 0)
        want = jnp.where(pick == 0, times_ref[0], times_ref[1])
        hot = jnp.where(jnp.logical_and(pick < 2, ids == want), 1.0, 0.0).astype(BF)
        trow[...] = dot_nn(hot, dpk[pl.ds(0, table_rows), :])
        for mb in range(2):

            def make(r):
                m = maskc[mb, r_rows(r), 0:1]
                base = jnp.where(m > 0.5, vector_ref[...], outb[mb, r_rows(r), :].astype(F32))
                h[mb, r_rows(r), :] = base + trow[mb : mb + 1, :]

            loop(parts_of, make)

    def first_half(mb, t):
        @pl.when(x1)
        def _():
            h[mb] = relay[mb].astype(F32)

        def ln(r):
            xhat, _ = norm_parts(h[mb, r_rows(r), :])
            normed[sub_rows(mb, r), :] = (xhat * gains_ref[0:1, :]).astype(BF)

        loop(parts_of, ln)

        @pl.when(jnp.logical_and(x0, t == 0))
        def _():
            loop(6, gather_step)
            for i in (9, 10, 11, 8):
                near_ready(i)
                far_ready(i)

        def qkv(k):
            packed[k, seq_rows(mb), :] = dot_nn(normed[seq_rows(mb), :], chunk(QKV0 + k)).astype(BF)

        loop(3, qkv)

        @pl.when(x0)
        def _():
            gather_step(6 + 2 * t)

        def attend(j):
            cols = pl.ds(pl.multiple_of(j * 128, 128), 128)
            q2 = packed[0, seq_rows(mb), cols]
            k2 = packed[1, seq_rows(mb), cols]
            v2 = packed[2, seq_rows(mb), cols]
            total = jnp.zeros((seq, 128), F32)
            for e in range(2):
                sc = dot_nt(q2 * scaled[e], k2)
                ex = jnp.exp(sc - jnp.max(sc, axis=-1, keepdims=True))
                pr = (ex / jnp.sum(ex, axis=-1, keepdims=True)).astype(BF)
                probs[mb, 2 * j + e] = pr
                total = total + dot_nn(pr, v2 * masks[e])
            mixed[seq_rows(mb), cols] = total.astype(BF)

        loop(HEADS // 2, attend)

        @pl.when(x0)
        def _():
            gather_step(7 + 2 * t)

        mid[mb] = h[mb] + dot_nn(mixed[seq_rows(mb), :], chunk(PROJ))

        def ln_two(r):
            xhat, _ = norm_parts(mid[mb, r_rows(r), :])
            n2[sub_rows(mb, r), :] = (xhat * gains_ref[1:2, :]).astype(BF)

        loop(parts_of, ln_two)

    def mlp_up(q, mb):
        up = dot_nn(n2[seq_rows(mb), :], chunk(IN0 + q))
        sq = up * up
        t = jnp.tanh(GELU_C * up * (1.0 + 0.044715 * sq))
        hp = 0.5 * (1.0 + t)
        actv[q, seq_rows(mb), :] = (up * hp).astype(BF)
        gp[q, seq_rows(mb), :] = (hp + (0.5 * GELU_C) * up * (1.0 - t * t) * (1.0 + 0.134145 * sq)).astype(BF)

    def mlp_down(q, mb):
        acc[mb] += dot_nn(actv[q, seq_rows(mb), :], chunk(OUT0 + q))

    def second_half(base, number):
        @pl.when(x0)
        def _():
            for i in range(IN0, PROJ):
                near_ready(i)
                far_ready(i)

        def up(i):
            mlp_up(i // number, base + lax.rem(i, number))

        loop(4 * number, up)

        def init(i):
            acc[base + i] = mid[base + i]

        loop(number, init)

        def down(i):
            mlp_down(lax.rem(2 * y + i // number, 4), base + lax.rem(i, number))

        @pl.when(x0)
        def _():
            gather_step(10)
            gather_step(11)
            for i in range(IN0):
                near_ready(i)

        loop(2 * number, down)

        @pl.when(x0)
        def _():
            gather_step(12)
            gather_step(13)
            for i in range(IN0):
                far_ready(i)

        loop(2 * number, lambda i: down(2 * number + i))

        def finish(i):
            outb[base + i] = acc[base + i].astype(BF)

        loop(number, finish)

    def relay_copy(mb, part):
        r = pl.ds(part * (seq // 2), seq // 2)
        return remote(
            outb.at[mb, r], relay.at[mb, r], rsend.at[mb, part], rrecv.at[mb, part], {"section": 1 - s}
        )

    def act_copy(mb):
        return pltpu.make_async_copy(outb.at[mb], act_out.at[mb], osem.at[0, mb])

    def dx_copy(mb):
        return pltpu.make_async_copy(h.at[mb], dx_out.at[mb], osem.at[1, mb])

    def norm_back(v, gain, dy):
        xhat, inv = norm_parts(v)
        dxh = dy * gain
        m1 = jnp.mean(dxh, axis=-1, keepdims=True)
        m2 = jnp.mean(dxh * xhat, axis=-1, keepdims=True)
        return inv * (dxh - m1 - xhat * m2), jnp.sum(dy * xhat, axis=0, keepdims=True)

    def backward_mlp(mb):
        @pl.when(x0)
        def _():
            glow[seq_rows(mb), :] = relay[mb]

        @pl.when(x1)
        def _():
            cot_copy(mb).wait()

        tmp[...] = jnp.zeros_like(tmp)

        def mlp(q):
            da = dot_nt(glow[seq_rows(mb), :], chunk(OUT0 + q))
            du = (gp[q, seq_rows(mb), :].astype(F32) * da).astype(BF)
            gp[q, seq_rows(mb), :] = du
            tmp[...] += dot_nt(du, chunk(IN0 + q))

        loop(4, mlp)

        def ln_two(r):
            dx, dg = norm_back(mid[mb, r_rows(r), :], gains_ref[1:2, :], tmp[r_rows(r), :])
            dm = glow[sub_rows(mb, r), :].astype(F32) + dx
            acc[mb, r_rows(r), :] = dm
            dmlow[sub_rows(mb, r), :] = dm.astype(BF)
            gains_acc[1:2, :] += dg

        loop(parts_of, ln_two)

    def backward_attention(mb):
        do_ref[...] = dot_nt(dmlow[seq_rows(mb), :], chunk(PROJ)).astype(BF)

        def attend(j):
            cols = pl.ds(pl.multiple_of(j * 128, 128), 128)
            q2 = packed[0, seq_rows(mb), cols]
            k2 = packed[1, seq_rows(mb), cols]
            v2 = packed[2, seq_rows(mb), cols]
            do2 = do_ref[:, cols]
            dq = jnp.zeros((seq, 128), F32)
            dk = jnp.zeros((seq, 128), F32)
            dv = jnp.zeros((seq, 128), F32)
            for e in range(2):
                pr = probs[mb, 2 * j + e]
                dom = do2 * masks[e]
                dp = dot_nt(dom, v2)
                pf = pr.astype(F32)
                inner = jnp.sum(dp * pf, axis=-1, keepdims=True)
                ds = (pf * (dp - inner)).astype(BF)
                dv = dv + dot_tn(pr, dom)
                dq = dq + dot_nn(ds, k2 * scaled[e])
                dk = dk + dot_tn(ds, q2 * scaled[e])
            for k, v in enumerate((dq, dk, dv)):
                dpk[rows(k * 2 * seq + mb * seq, seq, seq), cols] = v.astype(BF)

        loop(HEADS // 2, attend)
        tmp[...] = jnp.zeros_like(tmp)

        def qkv(k):
            tmp[...] += dot_nt(dpk[rows(k * 2 * seq + mb * seq, seq, seq), :], chunk(QKV0 + k))

        loop(3, qkv)

        for part in range(2):

            def ln_one(rr):
                r = rr + part * (parts_of // 2)
                dx, dg = norm_back(h[mb, r_rows(r), :], gains_ref[0:1, :], tmp[r_rows(r), :])
                dm = acc[mb, r_rows(r), :] + dx
                outb[mb, r_rows(r), :] = dm.astype(BF)
                gains_acc[0:1, :] += dg
                m = maskc[mb, r_rows(r), 0:1]
                kept = jnp.where(jnp.logical_and(x0, m > 0.5), 0.0, dm)
                h[mb, r_rows(r), :] = kept
                pay[pl.ds(2 + mb, 1), 0:width] += jnp.sum(dm, axis=0, keepdims=True)
                pay[4:5, 0:width] += jnp.sum(dm - kept, axis=0, keepdims=True)

            loop(parts_of // 2, ln_one)

            @pl.when(x1)
            def _():
                relay_copy(mb, part).start()

        dx_copy(mb).start()

    def grad_chunk(a, b, k):
        w[rows(k * width, width, width), :] = dot_tn(a, b).astype(BF)

    def cslot(i, yy):
        return cbuf.at[yy, rows(i * quarter, quarter, quarter)]

    def to_twin(i, yy):
        q = 2 * yy + (1 - c)
        return remote(
            w.at[rows(place(i, q), quarter, quarter)], cslot(i, yy), csend.at[yy, i], crecv.at[yy, i], {"grp": twin}
        )

    def urows(u):
        return rows(u * unit, unit, unit)

    def y_send(u):
        return remote(
            cbuf.at[1 - y, urows(u)], ybuf.at[urows(u)], usend.at[0, u], urecv.at[0, u], {"grp": across}
        )

    def publish(first, number):
        def send(j):
            for yy in range(2):
                to_twin(first + j, yy).start()

        loop(number, send)

        def merge(j):
            i = first + j
            for yy in range(2):
                to_twin(i, yy).wait_recv()
            for yy in range(2):
                old = cbuf[yy, rows(i * quarter, quarter, quarter), :].astype(F32)
                mine = w[rows(place(i, 2 * yy + c), quarter, quarter), :].astype(F32)
                cbuf[yy, rows(i * quarter, quarter, quarter), :] = (old + mine).astype(BF)
            loop(per_block, lambda m: y_send(i * per_block + m).start())

        loop(number, merge)

    def mlp_grads():
        loop(4, lambda q: grad_chunk(actv[q], glow[...], OUT0 + q))
        publish(OUT0, 4)
        loop(4, lambda q: grad_chunk(n2[...], gp[q], IN0 + q))
        publish(IN0, 4)

    def attention_grads():
        grad_chunk(mixed[...], dmlow[...], PROJ)
        loop(3, lambda k: grad_chunk(normed[...], dpk[rows(k * 2 * seq, 2 * seq, 2 * seq), :], QKV0 + k))
        publish(PROJ, 4)

    def step(t):
        mb = jnp.where(x0, lax.rem(t, 2), t // 2)
        is_f = jnp.where(x0, t < 2, lax.rem(t, 2) == 0)

        @pl.when(is_f)
        def _():
            @pl.when(x1)
            def _():
                relay_copy(mb, 0).wait_recv()
                relay_copy(mb, 1).wait_recv()

            first_half(mb, t)

            @pl.when(jnp.logical_or(x1, t == 1))
            def _():
                second_half(jnp.where(x0, 0, mb), jnp.where(x0, 2, 1))

                @pl.when(x0)
                def _():
                    for b in range(2):
                        relay_copy(b, 0).start()
                        relay_copy(b, 1).start()
                        act_copy(b).start()

                @pl.when(x1)
                def _():
                    act_copy(mb).start()

        @pl.when(jnp.logical_not(is_f))
        def _():
            act_copy(mb).wait()

            @pl.when(x0)
            def _():
                for part in range(2):
                    relay_copy(mb, part).wait_send()
                    relay_copy(mb, part).wait_recv()

            backward_mlp(mb)

            @pl.when(jnp.logical_and(x0, t == 3))
            def _():
                gather_sent()
                mlp_grads()

            backward_attention(mb)

    def gather_sent():
        for i in range(CHUNKS):
            own_across(i).wait_send()
            own_to_twin(i).wait_send()
            y_to_z(i).wait_send()
            y_to_twin(i).wait_send()
            z_to_twin(i).wait_send()

    @pl.when(x1)
    def _():
        loop(gather_steps, gather_step)
        for i in range(CHUNKS):
            near_ready(i)
            far_ready(i)

    loop(4, step)

    @pl.when(x1)
    def _():
        gather_sent()
        mlp_grads()

    attention_grads()

    pay[0:2, 0:width] = gains_acc[0:2, :]
    for mb in range(2):
        pay[2 + mb : 3 + mb, pl.ds(width, 128)] = jnp.full((1, 128), times_ref[mb].astype(F32))
    for r in (0, 1, 4, 5, 6, 7):
        pay[r : r + 1, pl.ds(width, 128)] = jnp.full((1, 128), -1.0, F32)

    def add_rows(dst, dst_rows, a, b):
        dst[dst_rows, :] = (a.astype(F32) + b.astype(F32)).astype(BF)

    if nz == 4:
        end = jnp.logical_or(d == 0, d == 3)
        inner = jnp.logical_not(end)
        slots, pay_in = extra

        def slot_copy(k):
            first, size, peer = (
                (d * 4 + g, 1, {"grp": twin}),
                (d * 4 + 2 * y, 2, {"grp": across}),
                (d * 4, 4, {"dp": zpair}),
                ((d // 2) * 8, 8, {"dp": zfar}),
            )[k]
            ref = slots.at[rows(first * 8, size * 8, 8)]
            return remote(ref, ref, psend.at[1 + k], precv.at[1 + k], peer)

        def slot_wait(k):
            first, size, peer = (
                (d * 4 + twin, 1, {"grp": twin}),
                (d * 4 + 2 * (1 - y), 2, {"grp": across}),
                (zpair * 4, 4, {"dp": zpair}),
                ((1 - d // 2) * 8, 8, {"dp": zfar}),
            )[k]
            ref = slots.at[rows(first * 8, size * 8, 8)]
            remote(ref, ref, psend.at[1 + k], precv.at[1 + k], peer).wait_recv()

        pay_copy = remote(pay, pay_in, psend.at[0], precv.at[0], {"section": 1 - s})

        @pl.when(x0)
        def _():
            pay_copy.start()

        def small_start():
            @pl.when(x1)
            def _():
                pay_copy.wait_recv()
                pay[2:8, :] = pay_in[2:8, :]

            slots[rows((d * 4 + g) * 8, 8, 8), :] = pay[...]
            slot_copy(0).start()

        def small_next(k):
            slot_wait(k)
            slot_copy(k + 1).start()

        def small_end():
            slot_wait(3)
            total = slots[0:8, :]
            for k in range(1, 16):
                total = total + slots[k * 8 : k * 8 + 8, :]
            shard = s * 4 + g
            small_out[0:8, :] = pltpu.roll(total[:, 0:width], lax.rem(width - quarter * g, width), 1)
            small_out[8:16, :] = pltpu.roll(
                total[:, 0:width], lax.rem(width - (width // 8) * shard, width), 1
            )
            base = shard * (table_rows // 8)
            ids = (base + lax.broadcasted_iota(jnp.int32, (128, 128), 1)).astype(F32)
            pick = jnp.where(slots[:, pl.ds(width, 128)] == ids, 1.0, 0.0)
            table_out[...] = lax.dot_general(
                pick,
                slots[:, 0:width],
                (((0,), (0,)), ((), ())),
                precision=lax.Precision.HIGHEST,
                preferred_element_type=F32,
            )

        def end_to_inner(u):
            return remote(
                ybuf.at[urows(u)], z1.at[urows(u)], usend.at[1, u], urecv.at[1, u], {"dp": zpair}
            )

        def inner_swap(u):
            return remote(
                z1.at[urows(u)], z2.at[urows(u)], usend.at[2, u], urecv.at[2, u], {"dp": 3 - d}
            )

        def inner_to_end(u):
            return remote(
                z2.at[urows(u)], z1.at[urows(u)], usend.at[1, u], urecv.at[1, u], {"dp": zpair}
            )

        def out_end(u):
            return pltpu.make_async_copy(z1.at[urows(u)], grad_out.at[urows(u)], usend.at[2, u])

        def out_inner(u):
            return pltpu.make_async_copy(z2.at[urows(u)], grad_out.at[urows(u)], urecv.at[3, u])

        lag3, lag4, lag5 = 2, 4, 6
        first_small = 12

        def tick(t):
            u2, u3, u4, u5 = t, t - lag3, t - lag4, t - lag5

            @pl.when(u2 < units)
            def _():
                y_send(u2).wait_recv()
                add_rows(ybuf, urows(u2), cbuf[y, urows(u2), :], ybuf[urows(u2), :])

                @pl.when(end)
                def _():
                    end_to_inner(u2).start()

            @pl.when(jnp.logical_and(inner, jnp.logical_and(u3 >= 0, u3 < units)))
            def _():
                end_to_inner(u3).wait_recv()
                add_rows(z1, urows(u3), ybuf[urows(u3), :], z1[urows(u3), :])
                inner_swap(u3).start()

            @pl.when(jnp.logical_and(inner, jnp.logical_and(u4 >= 0, u4 < units)))
            def _():
                inner_swap(u4).wait_recv()
                add_rows(z2, urows(u4), z1[urows(u4), :], z2[urows(u4), :])
                inner_to_end(u4).start()
                out_inner(u4).start()

            @pl.when(jnp.logical_and(end, jnp.logical_and(u5 >= 0, u5 < units)))
            def _():
                inner_to_end(u5).wait_recv()
                out_end(u5).start()

            pl.when(t == first_small)(small_start)
            for k in range(3):
                pl.when(t == first_small + 2 + 2 * k)(functools.partial(small_next, k))
            pl.when(t == first_small + 8)(small_end)

        loop(units + lag5, tick)

        def drain(u):
            y_send(u).wait_send()

            @pl.when(end)
            def _():
                end_to_inner(u).wait_send()
                out_end(u).wait()

            @pl.when(inner)
            def _():
                inner_swap(u).wait_send()
                inner_to_end(u).wait_send()
                out_inner(u).wait()

        loop(units, drain)

        @pl.when(x0)
        def _():
            pay_copy.wait_send()

        for k in range(4):
            slot_copy(k).wait_send()
    else:
        small_out[...] = pay[...]
        table_out[...] = jnp.zeros_like(table_out)

        def out_sum(u):
            return pltpu.make_async_copy(ybuf.at[urows(u)], grad_out.at[urows(u)], usend.at[1, u])

        def tick(u):
            y_send(u).wait_recv()
            add_rows(ybuf, urows(u), cbuf[y, urows(u), :], ybuf[urows(u), :])
            out_sum(u).start()

        loop(units, tick)

        def drain(u):
            y_send(u).wait_send()
            out_sum(u).wait()

        loop(units, drain)

    def sent(i):
        for yy in range(2):
            to_twin(i, yy).wait_send()

    loop(CHUNKS, sent)
    for mb in range(2):
        dx_copy(mb).wait()

        @pl.when(x1)
        def _():
            for part in range(2):
                relay_copy(mb, part).wait_send()


def run_mega(timesteps, mask_flags, vector, gains, emb, cot, table, wq, wp, wi, wo, nz):
    count, seq, width = emb.shape
    quarter = wp.shape[0]
    unit = quarter // 2
    units = CHUNKS * quarter // unit
    tokens = count * seq
    assert count == 2 and quarter * 4 == width and wi.shape[1] == 4 * width and wo.shape[0] == width
    vmem = pl.BlockSpec(memory_space=pltpu.VMEM)
    smem = pl.BlockSpec(memory_space=pltpu.SMEM)
    hbm = pl.BlockSpec(memory_space=pl.ANY)
    dma = pltpu.SemaphoreType.DMA
    small = (16, width) if nz == 4 else (8, width + 128)
    extra = [pltpu.VMEM((nz * 4 * 8, width + 128), F32), pltpu.VMEM((8, width + 128), F32)]
    return pl.pallas_call(
        functools.partial(mega, (count, seq, width, nz, unit)),
        out_shape=(
            jax.ShapeDtypeStruct((count, seq, width), BF),
            jax.ShapeDtypeStruct((count, seq, width), F32),
            jax.ShapeDtypeStruct((CHUNKS * quarter, width), BF),
            jax.ShapeDtypeStruct(small, F32),
            jax.ShapeDtypeStruct((128, width), F32),
        ),
        in_specs=[smem, vmem, vmem, vmem] + [hbm] * 7,
        out_specs=(hbm, hbm, hbm, vmem, vmem),
        scratch_shapes=[
            pltpu.VMEM((CHUNKS * width, width), BF),
            pltpu.VMEM((count, seq, width), F32),
            pltpu.VMEM((count, seq, width), F32),
            pltpu.VMEM((count, seq, width), F32),
            pltpu.VMEM((seq, width), F32),
            pltpu.VMEM((tokens, width), BF),
            pltpu.VMEM((tokens, width), BF),
            pltpu.VMEM((tokens, width), BF),
            pltpu.VMEM((4, tokens, width), BF),
            pltpu.VMEM((4, tokens, width), BF),
            pltpu.VMEM((3, tokens, width), BF),
            pltpu.VMEM((count, HEADS, seq, seq), BF),
            pltpu.VMEM((tokens, width), BF),
            pltpu.VMEM((tokens, width), BF),
            pltpu.VMEM((3 * tokens, width), BF),
            pltpu.VMEM((seq, width), BF),
            pltpu.VMEM((count, seq, width), BF),
            pltpu.VMEM((count, seq, width), BF),
            pltpu.VMEM((count, seq, 128), F32),
            pltpu.VMEM((8, width), F32),
            pltpu.VMEM((8, width + 128), F32),
            pltpu.VMEM((8, width), F32),
            pltpu.VMEM((2, CHUNKS * quarter, width), BF),
            pltpu.VMEM((CHUNKS * quarter, width), BF),
            pltpu.VMEM((CHUNKS * quarter, width), BF),
            pltpu.VMEM((CHUNKS * quarter, width), BF),
            dma((4,)),
            dma((CHUNKS,)),
            dma((5, CHUNKS)),
            dma((5, CHUNKS)),
            dma((2, 2)),
            dma((2, 2)),
            dma((2, CHUNKS)),
            dma((2, CHUNKS)),
            dma((3, units)),
            dma((4, units)),
            dma((5,)),
            dma((5,)),
            dma((2, 2)),
        ]
        + (extra if nz == 4 else []),
        compiler_params=pltpu.CompilerParams(
            collective_id=0, has_side_effects=True, vmem_limit_bytes=67043328
        ),
        name="relay_layers",
    )(timesteps, mask_flags, vector, gains, emb, cot, table, wq, wp, wi, wo)


def small_sums(sizes, small, timesteps, rows_count, quarter):
    ns, ng, nz = sizes
    width = quarter * 4
    section, member = lax.axis_index("section"), lax.axis_index("grp")
    every = lax.all_gather(small, ("section", "grp", "dp"), axis=0, tiled=False)
    per_plane = every.reshape(ns, ng * nz, 8, width + 128)
    mine = lax.dynamic_index_in_dim(per_plane, section, 0, keepdims=False)[:, :2, :width].sum(axis=0)
    grad_gains = lax.dynamic_slice(mine, (0, member * quarter), (2, quarter))
    shard = section * ng + member
    here = rows_count // (ns * ng)
    ids = (shard * here + jnp.arange(here)).astype(F32)
    stamp = per_plane[0, :, :, width].reshape(-1)
    pick = (ids[:, None] == stamp[None, :]).astype(F32)
    grad_table = jnp.dot(pick, per_plane[0, :, :, :width].reshape(-1, width), precision=lax.Precision.HIGHEST)
    mask_here = width // (ns * ng)
    grad_mask = lax.dynamic_slice(per_plane[0, :, 4, :width].sum(axis=0), (shard * mask_here,), (mask_here,))
    return grad_gains, grad_table, grad_mask


def on_device(
    sizes,
    embeddings,
    mask_flags,
    timesteps,
    time_table,
    mask_vector,
    attn_qkv,
    attn_out,
    mlp_in,
    mlp_out,
    norm_gains,
    cotangent,
):
    ns, ng, nz = sizes
    rows_count, width = time_table.shape
    activations, dx, grads, small, table = run_mega(
        timesteps,
        mask_flags,
        mask_vector.astype(F32)[None],
        norm_gains[0],
        embeddings,
        cotangent,
        time_table,
        attn_qkv[0],
        attn_out[0],
        mlp_in[0],
        mlp_out[0],
        nz,
    )
    quarter = attn_out.shape[1]
    if nz == 4:
        grad_gains = small[:2, :quarter]
        grad_table = table[: rows_count // (ns * ng)]
        grad_mask = small[12, : width // (ns * ng)]
    else:
        grads = lax.psum(grads, "dp")
        grad_gains, grad_table, grad_mask = small_sums(sizes, small, timesteps, rows_count, quarter)

    def blocks(first, n):
        return jnp.concatenate(
            [grads[(first + j) * quarter : (first + j + 1) * quarter] for j in range(n)], axis=1
        ).astype(F32)

    return (
        activations[None],
        dx[None],
        blocks(QKV0, 3)[None],
        blocks(PROJ, 1)[None],
        blocks(IN0, 4)[None],
        grads[: 4 * quarter].astype(F32)[None],
        grad_gains[None],
        grad_table,
        grad_mask,
    )


def solution(mesh):
    sizes = (mesh.shape["section"], mesh.shape["grp"], mesh.shape["dp"])
    placed = (
        P(("grp", "dp"), None, None),
        P(("grp", "dp"), None),
        P(("grp", "dp")),
        P(),
        P(),
        P("section", "grp", None),
        P("section", "grp", None),
        P("section", "grp", None),
        P("section", "grp", None),
        P("section", None, None),
        P(("grp", "dp"), None, None),
    )
    return jax.shard_map(
        functools.partial(on_device, sizes),
        mesh=mesh,
        in_specs=placed,
        out_specs=(
            P("section", ("grp", "dp"), None, None),
            P("section", ("grp", "dp"), None, None),
            P("section", "grp", None),
            P("section", "grp", None),
            P("section", "grp", None),
            P("section", "grp", None),
            P("section", None, "grp"),
            P(("section", "grp"), None),
            P(("section", "grp")),
        ),
        check_vma=False,
    )
```

time: 657 us -> 284 us (0.43); the launches traced: 650 us -> 284 us
  waiting for transfers between devices: 366 us -> 0 us
  Pallas kernels: 0 us -> 270 us
  matrix products: 141 us -> 0 us
  blocking collectives: 51.9 us -> 0 us
  local copies, waits for them, and re-layouts: 28.4 us -> 6.68 us
  other arithmetic: 28.3 us -> 6.99 us
  between operations: 17.8 us -> 0.66 us
  starting transfers between devices: 16.9 us -> 0 us
    pallas_call x0 -> x1, Pallas kernels: none -> 270 us  [run_mega(): pl.pallas_call(functools.partial(mega, (count, seq, width, nz, unit)), ou...]
    dot_general x53 -> x0, matrix products: 132 us -> none  [the longest x12 46.1 us: contract_rows(): lax.dot_general(left, right, (((0,), (0,)), ((), ())), preferred_element_...]
    psum x1 -> x0, waiting for transfers between devices: 130 us -> none  [on_device(): lax.psum(shards[0].astype(jnp.bfloat16), 'dp').astype(jnp.float32)]
    all_gather x4 -> x0, waiting for transfers between devices: 111 us -> none  [the longest x1 36.9 us: on_device(): lax.all_gather(mlp_in[0], 'grp', axis=0, tiled=True)]
    reduce_scatter x4 -> x0, waiting for transfers between devices: 94.5 us -> none  [the longest x1 50.5 us: on_device(): lax.psum_scatter(acc_terms[3][None].astype(jnp.bfloat16), 'grp', scatter_...]
    unnamed x2 -> x0, blocking collectives: 40.1 us -> none
    ppermute x4 -> x0, waiting for transfers between devices: 27.2 us -> none  [from_behind(): return lax.ppermute(value, axis, pairs)]
    unnamed x245 -> x11, local copies, waits for them, and re-layouts: 15.8 us -> 2.95 us
  transfers between devices with their start and end apart: 15 -> 0, of which waited for: 12 -> 0; matrix products, arithmetic and copies ran while one was open for 17% -> 0% of each run, Pallas kernels for 0% -> 0%
where the time goes in v1:
time: 284 us
  Pallas kernels  270 us (95%)
  other arithmetic  6.99 us (2%)
  local copies, waits for them, and re-layouts  6.68 us (2%)
    pallas_call x1, Pallas kernels, run_mega(): pl.pallas_call(functools.partial(mega, (count, seq, width, nz, unit)), ou...  270 us

profile of v1, /device:TPU:0, one launch (start us, length us, event | category | flops | bytes accessed | tf_op | source)
XLA Modules:
  0.0 284.0 jit_solution(8982744816598615604)
XLA Ops:
  0.6 1.3 reshape.115.vector_ref
  1.9 269.6 %relay_layers.1 = (bf16[2,256,768]{2,1,0:T(8,128)(2,1)}, f32[2,256,768]{2,1,0:T(8,128)}, bf16[2304,768]{1,0:T(8,128)(2,1)}, f32[16,768]{1,0:T(8,128)}, f32[128,768]{1,0:T(8,128)}) custom-call(s32[2]{0:T(128)} %times_ref.1, s32[2,256]{1,0:T(2,128)} %mask_ref.1, f32[1,768]{1,0:T(1,128)} %reshape.115.vector_ref, f32[2,768]{1,0:T(2,128)} %bitcast.39, ...), custom_call_target="tpu_custom_call" | custom-call | tf_op jit(solution)/shard_map/relay_layers/pallas_call | solution.py:824
  271.5 1.2 slice_bitcast_fusion.8
  272.7 1.3 slice_bitcast_fusion.7
  274.0 0.0 copy-start
  274.0 3.0 %bitcast_convert_fusion = f32[1,768,768]{2,1,0:T(8,128)} fusion(bf16[2304,768]{1,0:T(8,128)(2,1)} %get-tuple-element.16), kind=kLoop, calls=%fused_computation.1 | loop fusion | flops 589824 | bytes 3538944 | tf_op jit(solution)/shard_map/broadcast_in_dim | solution.py:953
  277.0 0.0 copy-done
  277.0 1.0 slice_bitcast_fusion.3
  278.0 1.7 maximum_convert_fusion
  279.7 0.0 copy-start.2
  279.7 0.0 copy-start.1
  279.7 1.3 maximum_convert_fusion.1
  281.0 0.1 copy-done.2
  281.1 0.9 copy.23
  282.0 0.0 copy-done.1
  282.0 0.0 copy-start.3
  282.0 1.1 copy.24
  283.1 0.1 copy-done.3
  283.2 0.7 copy.25
Async XLA Ops:
  274.0 3.0 %copy-start = (bf16[2304,768]{1,0:T(8,128)(2,1)S(1)}, bf16[2304,768]{1,0:T(8,128)(2,1)}, u32[]{:S(2)}) copy-start(bf16[2304,768]{1,0:T(8,128)(2,1)} %get-tuple-element.16) | copy-start | bytes 10616836
  279.7 1.4 copy-start.2
  279.7 2.3 copy-start.1
  282.0 1.2 copy-start.3

commit v2 on v1

--- a/solution.py
+++ b/solution.py
@@ -32,8 +32,13 @@
     return lax.dot_general(a, b, (((0,), (0,)), ((), ())), preferred_element_type=F32)
 
 
-def loop(n, body):
-    lax.fori_loop(0, n, lambda i, c: (body(i), c)[1], 0)
+def loop(n, body, first=0):
+    lax.fori_loop(first, n, lambda i, c: (body(i), c)[1], 0)
+
+
+def unrolled(n, body):
+    for i in range(n):
+        body(i)
 
 
 def mega(
@@ -59,6 +64,7 @@
     mid,
     acc,
     tmp,
+    inv_sum,
     normed,
     mixed,
     n2,
@@ -240,9 +246,10 @@
     def chunk(k):
         return w[rows(k * width, width, width), :]
 
-    step_rows = 64
+    step_rows = 32
     parts_of = seq // step_rows
     lane = lax.broadcasted_iota(jnp.int32, (1, 128), 1)
+    low_lane = lax.broadcasted_iota(jnp.int32, (seq, 128), 1) < HEAD
     low_half = (lane < HEAD).astype(F32)
     masks = (low_half.astype(BF), (1.0 - low_half).astype(BF))
     scaled = ((low_half * 0.125).astype(BF), ((1.0 - low_half) * 0.125).astype(BF))
@@ -261,6 +268,13 @@
         spread = jnp.mean(center * center, axis=-1, keepdims=True)
         inv = lax.rsqrt(spread + EPS)
         return center * inv, inv
+
+    @pl.when(x1)
+    def _():
+        loop(gather_steps, gather_step)
+        for i in range(CHUNKS):
+            near_ready(i)
+            far_ready(i)
 
     pay[...] = jnp.zeros_like(pay)
     gains_acc[...] = jnp.zeros_like(gains_acc)
@@ -294,7 +308,7 @@
             xhat, _ = norm_parts(h[mb, r_rows(r), :])
             normed[sub_rows(mb, r), :] = (xhat * gains_ref[0:1, :]).astype(BF)
 
-        loop(parts_of, ln)
+        unrolled(parts_of, ln)
 
         @pl.when(jnp.logical_and(x0, t == 0))
         def _():
@@ -313,20 +327,21 @@
             gather_step(6 + 2 * t)
 
         def attend(j):
-            cols = pl.ds(pl.multiple_of(j * 128, 128), 128)
+            cols = pl.ds(j * 128, 128)
             q2 = packed[0, seq_rows(mb), cols]
             k2 = packed[1, seq_rows(mb), cols]
             v2 = packed[2, seq_rows(mb), cols]
-            total = jnp.zeros((seq, 128), F32)
+            got = []
             for e in range(2):
                 sc = dot_nt(q2 * scaled[e], k2)
-                ex = jnp.exp(sc - jnp.max(sc, axis=-1, keepdims=True))
-                pr = (ex / jnp.sum(ex, axis=-1, keepdims=True)).astype(BF)
-                probs[mb, 2 * j + e] = pr
-                total = total + dot_nn(pr, v2 * masks[e])
-            mixed[seq_rows(mb), cols] = total.astype(BF)
-
-        loop(HEADS // 2, attend)
+                ex = jnp.exp(sc - jnp.max(sc, axis=-1, keepdims=True)).astype(BF)
+                probs[mb, 2 * j + e] = ex
+                got.append(dot_nn(ex, v2 * masks[e] + masks[1 - e]))
+            inv = 1.0 / pltpu.roll(jnp.where(low_lane, got[1], got[0]), HEAD, 1)
+            inv_sum[mb, :, cols] = inv
+            mixed[seq_rows(mb), cols] = (jnp.where(low_lane, got[0], got[1]) * inv).astype(BF)
+
+        unrolled(HEADS // 2, attend)
 
         @pl.when(x0)
         def _():
@@ -338,15 +353,17 @@
             xhat, _ = norm_parts(mid[mb, r_rows(r), :])
             n2[sub_rows(mb, r), :] = (xhat * gains_ref[1:2, :]).astype(BF)
 
-        loop(parts_of, ln_two)
+        unrolled(parts_of, ln_two)
 
     def mlp_up(q, mb):
         up = dot_nn(n2[seq_rows(mb), :], chunk(IN0 + q))
         sq = up * up
-        t = jnp.tanh(GELU_C * up * (1.0 + 0.044715 * sq))
-        hp = 0.5 * (1.0 + t)
-        actv[q, seq_rows(mb), :] = (up * hp).astype(BF)
-        gp[q, seq_rows(mb), :] = (hp + (0.5 * GELU_C) * up * (1.0 - t * t) * (1.0 + 0.134145 * sq)).astype(BF)
+        hp = 0.5 + 0.5 * jnp.tanh(up * (GELU_C + (GELU_C * 0.044715) * sq))
+        act = up * hp
+        actv[q, seq_rows(mb), :] = act.astype(BF)
+        gp[q, seq_rows(mb), :] = (
+            hp + act * ((1.0 - hp) * (2.0 * GELU_C + (2.0 * GELU_C * 0.134145) * sq))
+        ).astype(BF)
 
     def mlp_down(q, mb):
         acc[mb] += dot_nn(actv[q, seq_rows(mb), :], chunk(OUT0 + q))
@@ -361,6 +378,10 @@
         def up(i):
             mlp_up(i // number, base + lax.rem(i, number))
 
+            @pl.when(jnp.logical_and(x0, jnp.logical_or(i == 2, i == 5)))
+            def _():
+                gather_step(10 + i // 4)
+
         loop(4 * number, up)
 
         def init(i):
@@ -373,8 +394,6 @@
 
         @pl.when(x0)
         def _():
-            gather_step(10)
-            gather_step(11)
             for i in range(IN0):
                 near_ready(i)
 
@@ -413,7 +432,7 @@
         m2 = jnp.mean(dxh * xhat, axis=-1, keepdims=True)
         return inv * (dxh - m1 - xhat * m2), jnp.sum(dy * xhat, axis=0, keepdims=True)
 
-    def backward_mlp(mb):
+    def backward_mlp(mb, t):
         @pl.when(x0)
         def _():
             glow[seq_rows(mb), :] = relay[mb]
@@ -430,43 +449,52 @@
             gp[q, seq_rows(mb), :] = du
             tmp[...] += dot_nt(du, chunk(IN0 + q))
 
-        loop(4, mlp)
+        def mlp_and_out(k):
+            q = out_order(k)
+            mlp(q)
+            out_terms(k)
+
+        last = jnp.logical_and(x0, t == 3)
+        pl.when(last)(lambda: loop(4, mlp_and_out))
+        pl.when(jnp.logical_not(last))(lambda: loop(4, mlp))
 
         def ln_two(r):
             dx, dg = norm_back(mid[mb, r_rows(r), :], gains_ref[1:2, :], tmp[r_rows(r), :])
             dm = glow[sub_rows(mb, r), :].astype(F32) + dx
-            acc[mb, r_rows(r), :] = dm
+            mid[mb, r_rows(r), :] = dm
             dmlow[sub_rows(mb, r), :] = dm.astype(BF)
             gains_acc[1:2, :] += dg
 
-        loop(parts_of, ln_two)
-
-    def backward_attention(mb):
-        do_ref[...] = dot_nt(dmlow[seq_rows(mb), :], chunk(PROJ)).astype(BF)
+        unrolled(parts_of, ln_two)
+
+    def backward_attention(mb, t):
+        do_ref[...] = (dot_nt(dmlow[seq_rows(mb), :], chunk(PROJ)) * inv_sum[mb]).astype(BF)
 
         def attend(j):
-            cols = pl.ds(pl.multiple_of(j * 128, 128), 128)
+            cols = pl.ds(j * 128, 128)
             q2 = packed[0, seq_rows(mb), cols]
             k2 = packed[1, seq_rows(mb), cols]
             v2 = packed[2, seq_rows(mb), cols]
             do2 = do_ref[:, cols]
+            weighed = do2.astype(F32) * mixed[seq_rows(mb), cols].astype(F32)
             dq = jnp.zeros((seq, 128), F32)
             dk = jnp.zeros((seq, 128), F32)
             dv = jnp.zeros((seq, 128), F32)
             for e in range(2):
-                pr = probs[mb, 2 * j + e]
+                ex = probs[mb, 2 * j + e]
                 dom = do2 * masks[e]
-                dp = dot_nt(dom, v2)
-                pf = pr.astype(F32)
-                inner = jnp.sum(dp * pf, axis=-1, keepdims=True)
-                ds = (pf * (dp - inner)).astype(BF)
-                dv = dv + dot_tn(pr, dom)
+                inner = jnp.sum(jnp.where(low_lane if e == 0 else jnp.logical_not(low_lane), weighed, 0.0), axis=-1, keepdims=True)
+                ds = (ex.astype(F32) * (dot_nt(dom, v2) - inner)).astype(BF)
+                dv = dv + dot_tn(ex, dom)
                 dq = dq + dot_nn(ds, k2 * scaled[e])
                 dk = dk + dot_tn(ds, q2 * scaled[e])
             for k, v in enumerate((dq, dk, dv)):
                 dpk[rows(k * 2 * seq + mb * seq, seq, seq), cols] = v.astype(BF)
 
-        loop(HEADS // 2, attend)
+        for j in range(HEADS // 2):
+            attend(j)
+            if j % 3 == 2:
+                early_ticks(t, j // 3)
         tmp[...] = jnp.zeros_like(tmp)
 
         def qkv(k):
@@ -479,7 +507,7 @@
             def ln_one(rr):
                 r = rr + part * (parts_of // 2)
                 dx, dg = norm_back(h[mb, r_rows(r), :], gains_ref[0:1, :], tmp[r_rows(r), :])
-                dm = acc[mb, r_rows(r), :] + dx
+                dm = mid[mb, r_rows(r), :] + dx
                 outb[mb, r_rows(r), :] = dm.astype(BF)
                 gains_acc[0:1, :] += dg
                 m = maskc[mb, r_rows(r), 0:1]
@@ -488,7 +516,7 @@
                 pay[pl.ds(2 + mb, 1), 0:width] += jnp.sum(dm, axis=0, keepdims=True)
                 pay[4:5, 0:width] += jnp.sum(dm - kept, axis=0, keepdims=True)
 
-            loop(parts_of // 2, ln_one)
+            unrolled(parts_of // 2, ln_one)
 
             @pl.when(x1)
             def _():
@@ -516,116 +544,58 @@
             cbuf.at[1 - y, urows(u)], ybuf.at[urows(u)], usend.at[0, u], urecv.at[0, u], {"grp": across}
         )
 
-    def publish(first, number):
-        def send(j):
-            for yy in range(2):
-                to_twin(first + j, yy).start()
-
-        loop(number, send)
-
-        def merge(j):
-            i = first + j
-            for yy in range(2):
-                to_twin(i, yy).wait_recv()
-            for yy in range(2):
-                old = cbuf[yy, rows(i * quarter, quarter, quarter), :].astype(F32)
-                mine = w[rows(place(i, 2 * yy + c), quarter, quarter), :].astype(F32)
-                cbuf[yy, rows(i * quarter, quarter, quarter), :] = (old + mine).astype(BF)
-            loop(per_block, lambda m: y_send(i * per_block + m).start())
-
-        loop(number, merge)
-
-    def mlp_grads():
-        loop(4, lambda q: grad_chunk(actv[q], glow[...], OUT0 + q))
-        publish(OUT0, 4)
-        loop(4, lambda q: grad_chunk(n2[...], gp[q], IN0 + q))
-        publish(IN0, 4)
-
-    def attention_grads():
-        grad_chunk(mixed[...], dmlow[...], PROJ)
-        loop(3, lambda k: grad_chunk(normed[...], dpk[rows(k * 2 * seq, 2 * seq, 2 * seq), :], QKV0 + k))
-        publish(PROJ, 4)
-
-    def step(t):
-        mb = jnp.where(x0, lax.rem(t, 2), t // 2)
-        is_f = jnp.where(x0, t < 2, lax.rem(t, 2) == 0)
-
-        @pl.when(is_f)
-        def _():
-            @pl.when(x1)
-            def _():
-                relay_copy(mb, 0).wait_recv()
-                relay_copy(mb, 1).wait_recv()
-
-            first_half(mb, t)
-
-            @pl.when(jnp.logical_or(x1, t == 1))
-            def _():
-                second_half(jnp.where(x0, 0, mb), jnp.where(x0, 2, 1))
-
-                @pl.when(x0)
-                def _():
-                    for b in range(2):
-                        relay_copy(b, 0).start()
-                        relay_copy(b, 1).start()
-                        act_copy(b).start()
-
-                @pl.when(x1)
-                def _():
-                    act_copy(mb).start()
-
-        @pl.when(jnp.logical_not(is_f))
-        def _():
-            act_copy(mb).wait()
-
-            @pl.when(x0)
-            def _():
-                for part in range(2):
-                    relay_copy(mb, part).wait_send()
-                    relay_copy(mb, part).wait_recv()
-
-            backward_mlp(mb)
-
-            @pl.when(jnp.logical_and(x0, t == 3))
-            def _():
-                gather_sent()
-                mlp_grads()
-
-            backward_attention(mb)
-
-    def gather_sent():
-        for i in range(CHUNKS):
-            own_across(i).wait_send()
-            own_to_twin(i).wait_send()
-            y_to_z(i).wait_send()
-            y_to_twin(i).wait_send()
-            z_to_twin(i).wait_send()
-
-    @pl.when(x1)
-    def _():
-        loop(gather_steps, gather_step)
-        for i in range(CHUNKS):
-            near_ready(i)
-            far_ready(i)
-
-    loop(4, step)
-
-    @pl.when(x1)
-    def _():
-        gather_sent()
-        mlp_grads()
-
-    attention_grads()
-
-    pay[0:2, 0:width] = gains_acc[0:2, :]
-    for mb in range(2):
-        pay[2 + mb : 3 + mb, pl.ds(width, 128)] = jnp.full((1, 128), times_ref[mb].astype(F32))
-    for r in (0, 1, 4, 5, 6, 7):
-        pay[r : r + 1, pl.ds(width, 128)] = jnp.full((1, 128), -1.0, F32)
-
-    def add_rows(dst, dst_rows, a, b):
-        dst[dst_rows, :] = (a.astype(F32) + b.astype(F32)).astype(BF)
-
+    def merge_far(i):
+        to_twin(i, 1 - y).wait_recv()
+        part = rows(i * quarter, quarter, quarter)
+        mine = w[rows(place(i, 2 * (1 - y) + c), quarter, quarter), :].astype(F32)
+        cbuf[1 - y, part, :] = (cbuf[1 - y, part, :].astype(F32) + mine).astype(BF)
+
+    ahead = 6
+
+    def send_across(u):
+        pl.when(lax.rem(u, per_block) == 0)(lambda: merge_far(u // per_block))
+        y_send(u).start()
+
+    def out_order(k):
+        side = jnp.where(k < 2, 1 - y, y)
+        return 2 * side + jnp.where(lax.rem(k, 2) == 0, 1 - c, c)
+
+    def out_terms(k):
+        q = out_order(k)
+        grad_chunk(actv[q], glow[...], OUT0 + q)
+
+        @pl.when(lax.rem(k, 2) == 0)
+        def _():
+            loop(4, lambda i: to_twin(i, jnp.where(k == 0, 1 - y, y)).start())
+
+        @pl.when(k == 1)
+        def _():
+            loop(ahead, send_across)
+
+    def other_terms(i, a, b):
+        grad_chunk(a, b, i)
+        to_twin(i, 1 - y).start()
+        to_twin(i, y).start()
+
+    def in_terms():
+        loop(4, lambda q: other_terms(IN0 + q, n2[...], gp[q]))
+
+    def attention_terms():
+        other_terms(PROJ, mixed[...], dmlow[...])
+        loop(3, lambda k: other_terms(QKV0 + k, normed[...], dpk[rows(k * 2 * seq, 2 * seq, 2 * seq), :]))
+
+    def add_rows(dst, dst_rows, *terms):
+        dst[dst_rows, :] = functools.reduce(jnp.add, [a.astype(F32) for a in terms]).astype(BF)
+
+    def sum_across(u):
+        i = u // per_block
+        pl.when(lax.rem(u, per_block) == 0)(lambda: to_twin(i, y).wait_recv())
+        y_send(u).wait_recv()
+        mine = w[rows(place(i, g) + lax.rem(u, per_block) * unit, unit, unit), :]
+        add_rows(ybuf, urows(u), cbuf[y, urows(u), :], mine, ybuf[urows(u), :])
+
+    early = 4
+    early_count = 2 * early
     if nz == 4:
         end = jnp.logical_or(d == 0, d == 3)
         inner = jnp.logical_not(end)
@@ -652,10 +622,6 @@
             remote(ref, ref, psend.at[1 + k], precv.at[1 + k], peer).wait_recv()
 
         pay_copy = remote(pay, pay_in, psend.at[0], precv.at[0], {"section": 1 - s})
-
-        @pl.when(x0)
-        def _():
-            pay_copy.start()
 
         def small_start():
             @pl.when(x1)
@@ -682,14 +648,14 @@
             )
             base = shard * (table_rows // 8)
             ids = (base + lax.broadcasted_iota(jnp.int32, (128, 128), 1)).astype(F32)
-            pick = jnp.where(slots[:, pl.ds(width, 128)] == ids, 1.0, 0.0)
-            table_out[...] = lax.dot_general(
-                pick,
-                slots[:, 0:width],
-                (((0,), (0,)), ((), ())),
-                precision=lax.Precision.HIGHEST,
-                preferred_element_type=F32,
-            )
+            pick = jnp.where(slots[:, pl.ds(width, 128)] == ids, 1.0, 0.0).astype(BF)
+            rest = slots[:, 0:width]
+            found = jnp.zeros((128, width), F32)
+            for _ in range(3):
+                part = rest.astype(BF)
+                found = found + dot_tn(pick, part)
+                rest = rest - part.astype(F32)
+            table_out[...] = found
 
         def end_to_inner(u):
             return remote(
@@ -712,16 +678,17 @@
         def out_inner(u):
             return pltpu.make_async_copy(z2.at[urows(u)], grad_out.at[urows(u)], urecv.at[3, u])
 
-        lag3, lag4, lag5 = 2, 4, 6
-        first_small = 12
+        lag3, lag4, lag5 = 3, 6, 9
+        first_small = jnp.where(x0, early_count + 2, early_count + 12)
+        small_gap = 7
 
         def tick(t):
             u2, u3, u4, u5 = t, t - lag3, t - lag4, t - lag5
+            pl.when(u2 + ahead < units)(lambda: send_across(u2 + ahead))
 
             @pl.when(u2 < units)
             def _():
-                y_send(u2).wait_recv()
-                add_rows(ybuf, urows(u2), cbuf[y, urows(u2), :], ybuf[urows(u2), :])
+                sum_across(u2)
 
                 @pl.when(end)
                 def _():
@@ -747,10 +714,102 @@
 
             pl.when(t == first_small)(small_start)
             for k in range(3):
-                pl.when(t == first_small + 2 + 2 * k)(functools.partial(small_next, k))
-            pl.when(t == first_small + 8)(small_end)
-
-        loop(units + lag5, tick)
+                pl.when(t == first_small + small_gap * (k + 1))(functools.partial(small_next, k))
+            pl.when(t == first_small + small_gap * 4)(small_end)
+
+    else:
+
+        def out_sum(u):
+            return pltpu.make_async_copy(ybuf.at[urows(u)], grad_out.at[urows(u)], usend.at[1, u])
+
+        def tick(u):
+            pl.when(u + ahead < units)(lambda: send_across(u + ahead))
+            sum_across(u)
+            out_sum(u).start()
+
+    def early_ticks(t, k):
+        pl.when(jnp.logical_and(x0, t == 3))(lambda: loop((k + 1) * early, tick, k * early))
+
+    def step(t):
+        mb = jnp.where(x0, lax.rem(t, 2), t // 2)
+        is_f = jnp.where(x0, t < 2, lax.rem(t, 2) == 0)
+
+        @pl.when(is_f)
+        def _():
+            @pl.when(x1)
+            def _():
+                relay_copy(mb, 0).wait_recv()
+                relay_copy(mb, 1).wait_recv()
+
+            first_half(mb, t)
+
+            @pl.when(jnp.logical_or(x1, t == 1))
+            def _():
+                second_half(jnp.where(x0, 0, mb), jnp.where(x0, 2, 1))
+
+                @pl.when(x0)
+                def _():
+                    for b in range(2):
+                        relay_copy(b, 0).start()
+                        relay_copy(b, 1).start()
+                        act_copy(b).start()
+
+                @pl.when(x1)
+                def _():
+                    act_copy(mb).start()
+
+        @pl.when(jnp.logical_not(is_f))
+        def _():
+            act_copy(mb).wait()
+
+            @pl.when(x0)
+            def _():
+                for part in range(2):
+                    relay_copy(mb, part).wait_send()
+                    relay_copy(mb, part).wait_recv()
+
+            @pl.when(jnp.logical_and(x0, t == 3))
+            def _():
+                gather_sent()
+
+            backward_mlp(mb, t)
+
+            @pl.when(jnp.logical_and(x0, t == 3))
+            def _():
+                in_terms()
+
+            backward_attention(mb, t)
+
+    def gather_sent():
+        for i in range(CHUNKS):
+            own_across(i).wait_send()
+            own_to_twin(i).wait_send()
+            y_to_z(i).wait_send()
+            y_to_twin(i).wait_send()
+            z_to_twin(i).wait_send()
+
+    loop(4, step)
+
+    @pl.when(x1)
+    def _():
+        gather_sent()
+        loop(4, out_terms)
+        in_terms()
+
+    pay[0:2, 0:width] = gains_acc[0:2, :]
+    for mb in range(2):
+        pay[2 + mb : 3 + mb, pl.ds(width, 128)] = jnp.full((1, 128), times_ref[mb].astype(F32))
+    for r in (0, 1, 4, 5, 6, 7):
+        pay[r : r + 1, pl.ds(width, 128)] = jnp.full((1, 128), -1.0, F32)
+
+    if nz == 4:
+        pl.when(x0)(lambda: pay_copy.start())
+
+    attention_terms()
+
+    first_tick = jnp.where(x0, early_count, 0)
+    if nz == 4:
+        loop(units + lag5, tick, first_tick)
 
         def drain(u):
             y_send(u).wait_send()
@@ -777,16 +836,7 @@
     else:
         small_out[...] = pay[...]
         table_out[...] = jnp.zeros_like(table_out)
-
-        def out_sum(u):
-            return pltpu.make_async_copy(ybuf.at[urows(u)], grad_out.at[urows(u)], usend.at[1, u])
-
-        def tick(u):
-            y_send(u).wait_recv()
-            add_rows(ybuf, urows(u), cbuf[y, urows(u), :], ybuf[urows(u), :])
-            out_sum(u).start()
-
-        loop(units, tick)
+        loop(units, tick, first_tick)
 
         def drain(u):
             y_send(u).wait_send()
@@ -811,7 +861,7 @@
 def run_mega(timesteps, mask_flags, vector, gains, emb, cot, table, wq, wp, wi, wo, nz):
     count, seq, width = emb.shape
     quarter = wp.shape[0]
-    unit = quarter // 2
+    unit = quarter // 4
     units = CHUNKS * quarter // unit
     tokens = count * seq
     assert count == 2 and quarter * 4 == width and wi.shape[1] == 4 * width and wo.shape[0] == width
@@ -838,6 +888,7 @@
             pltpu.VMEM((count, seq, width), F32),
             pltpu.VMEM((count, seq, width), F32),
             pltpu.VMEM((seq, width), F32),
+            pltpu.VMEM((count, seq, width), F32),
             pltpu.VMEM((tokens, width), BF),
             pltpu.VMEM((tokens, width), BF),
             pltpu.VMEM((tokens, width), BF),

time: 284 us -> 247 us (0.87)
  Pallas kernels: 270 us -> 232 us
    pallas_call x1, Pallas kernels: 270 us -> 232 us  [run_mega(): pl.pallas_call(functools.partial(mega, (count, seq, width, nz, unit)), ou...]
where the time goes in v2:
time: 247 us
  Pallas kernels  232 us (94%)
  other arithmetic  6.99 us (3%)
  local copies, waits for them, and re-layouts  6.68 us (3%)
    pallas_call x1, Pallas kernels, run_mega(): pl.pallas_call(functools.partial(mega, (count, seq, width, nz, unit)), ou...  232 us

profile of v2, /device:TPU:0, one launch (start us, length us, event | category | flops | bytes accessed | tf_op | source)
XLA Modules:
  0.0 246.8 jit_solution(11447221036878668477)
XLA Ops:
  0.6 1.3 reshape.115.vector_ref
  1.9 232.5 %relay_layers.1 = (bf16[2,256,768]{2,1,0:T(8,128)(2,1)}, f32[2,256,768]{2,1,0:T(8,128)}, bf16[2304,768]{1,0:T(8,128)(2,1)}, f32[16,768]{1,0:T(8,128)}, f32[128,768]{1,0:T(8,128)}) custom-call(s32[2]{0:T(128)} %times_ref.1, s32[2,256]{1,0:T(2,128)} %mask_ref.1, f32[1,768]{1,0:T(1,128)} %reshape.115.vector_ref, f32[2,768]{1,0:T(2,128)} %bitcast.39, ...), custom_call_target="tpu_custom_call" | custom-call | tf_op jit(solution)/shard_map/relay_layers/pallas_call | solution.py:874
  234.4 1.2 slice_bitcast_fusion.8
  235.6 1.3 slice_bitcast_fusion.7
  236.9 0.0 copy-start
  236.9 3.0 %bitcast_convert_fusion = f32[1,768,768]{2,1,0:T(8,128)} fusion(bf16[2304,768]{1,0:T(8,128)(2,1)} %get-tuple-element.16), kind=kLoop, calls=%fused_computation.1 | loop fusion | flops 589824 | bytes 3538944 | tf_op jit(solution)/shard_map/broadcast_in_dim | solution.py:1004
  239.9 0.0 copy-done
  239.9 1.0 slice_bitcast_fusion.3
  240.9 1.7 maximum_convert_fusion
  242.5 0.0 copy-start.2
  242.5 0.0 copy-start.1
  242.5 1.3 maximum_convert_fusion.1
  243.9 0.1 copy-done.2
  243.9 0.9 copy.23
  244.8 0.0 copy-done.1
  244.8 0.0 copy-start.3
  244.8 1.1 copy.24
  246.0 0.1 copy-done.3
  246.1 0.7 copy.25
Async XLA Ops:
  236.9 3.0 %copy-start = (bf16[2304,768]{1,0:T(8,128)(2,1)S(1)}, bf16[2304,768]{1,0:T(8,128)(2,1)}, u32[]{:S(2)}) copy-start(bf16[2304,768]{1,0:T(8,128)(2,1)} %get-tuple-element.16) | copy-start | bytes 10616836
  242.5 1.4 copy-start.2
  242.5 2.3 copy-start.1
  244.8 1.2 copy-start.3

commit v3 on v2

v3 whole, which is shorter than its diff:
```python
import functools
import math

import jax
import jax.numpy as jnp
from jax import lax
from jax.experimental import pallas as pl
from jax.experimental.pallas import tpu as pltpu
from jax.sharding import PartitionSpec as P

HEADS = 12
HEAD = 64
BF = jnp.bfloat16
F32 = jnp.float32
MESH = pl.DeviceIdType.MESH
EPS = 1e-05
GELU_C = math.sqrt(2.0 / math.pi)

OUT0, IN0, PROJ, QKV0, CHUNKS = 0, 4, 8, 9, 12
YRING, ZRING = 16, 12
GATHER_ORDER = (9, 10, 11, 8, 4, 5, 6, 7, 0, 1, 2, 3)


def dot_nn(a, b):
    return lax.dot_general(a, b, (((1,), (0,)), ((), ())), preferred_element_type=F32)


def dot_nt(a, b):
    return lax.dot_general(a, b, (((1,), (1,)), ((), ())), preferred_element_type=F32)


def dot_tn(a, b):
    return lax.dot_general(a, b, (((0,), (0,)), ((), ())), preferred_element_type=F32)


def loop(n, body, first=0):
    lax.fori_loop(first, n, lambda i, c: (body(i), c)[1], 0)


def unrolled(n, body):
    for i in range(n):
        body(i)


def mega(
    cfg,
    times_ref,
    mask_ref,
    vector_ref,
    gains_ref,
    emb_hbm,
    cot_hbm,
    table_hbm,
    wq_hbm,
    wp_hbm,
    wi_hbm,
    wo_hbm,
    act_out,
    dx_out,
    grad_out,
    small_out,
    table_out,
    w,
    h,
    mid,
    acc,
    tmp,
    inv_sum,
    normed,
    mixed,
    n2,
    actv,
    gp,
    packed,
    probs,
    glow,
    dmlow,
    dpk,
    do_ref,
    outb,
    relay,
    maskc,
    trow,
    pay,
    sums,
    cbuf,
    ybuf,
    z1,
    z2,
    in_sem,
    own_sem,
    gsend,
    grecv,
    nrecv,
    rsend,
    rrecv,
    csend,
    crecv,
    ysend,
    yrecv,
    zsend,
    zrecv,
    zout,
    psend,
    precv,
    osem,
    *extra,
):
    count, seq, width, nz, unit = cfg
    quarter = width // 4
    units = CHUNKS * quarter // unit
    per_block = quarter // unit
    table_rows = table_hbm.shape[0]
    s = lax.axis_index("section")
    g = lax.axis_index("grp")
    d = lax.axis_index("dp")
    x0 = s == 0
    x1 = jnp.logical_not(x0)
    c = lax.rem(g, 2)
    y = g // 2
    twin = g + 1 - 2 * c
    across = lax.rem(g + 2, 4)
    zpair = d + 1 - 2 * lax.rem(d, 2)
    zfar = lax.rem(d + 2, 4)
    half = lax.rem(d, 2)

    peers = [{"section": 1 - s}, {"grp": twin}, {"grp": across}, {"dp": zpair}]
    if nz == 4:
        peers += [{"dp": 3 - d}, {"dp": zfar}]
    barrier = pltpu.get_barrier_semaphore()
    for peer in peers:
        pl.semaphore_signal(barrier, inc=1, device_id=peer, device_id_type=MESH)

    def remote(src, dst, send, recv, peer):
        return pltpu.make_async_remote_copy(
            src_ref=src, dst_ref=dst, send_sem=send, recv_sem=recv, device_id=peer, device_id_type=MESH
        )

    def rows(start, size, by):
        return pl.ds(pl.multiple_of(start, by), size)

    def place(i, q):
        return jnp.where(i < IN0, q * width + quarter * i, i * width + quarter * q)

    def source(i):
        if i < IN0:
            return wo_hbm.at[pl.ds(i * quarter, quarter)]
        if i < PROJ:
            return wi_hbm.at[:, pl.ds((i - IN0) * width, width)]
        if i == PROJ:
            return wp_hbm
        return wq_hbm.at[:, pl.ds((i - QKV0) * width, width)]

    sixth = quarter // 6
    share = {0: 2, 1: 3}
    far = across

    group_size = (4, 4, 1, 3)

    def group_of(i):
        if isinstance(i, int):
            return i // 4 if i < PROJ else 2 + (i > PROJ)
        return jnp.where(i < PROJ, i // 4, jnp.where(i == PROJ, 2, 3))

    def piece(i, q, first, n):
        return w.at[rows(place(i, q) + first * sixth, n * sixth, sixth)]

    def stage(k, i):
        return dpk.at[rows((k * CHUNKS + i) * sixth, sixth, sixth)]

    def own_copy(i):
        return pltpu.make_async_copy(source(i), w.at[rows(place(i, g), quarter, sixth)], own_sem.at[group_of(i)])

    def own_to_twin(i):
        return remote(source(i), w.at[rows(place(i, g), quarter, sixth)], gsend.at[0], nrecv.at[0, group_of(i)], {"grp": twin})

    def own_across(i, n):
        return remote(
            source(i).at[rows(half * n * sixth, n * sixth, sixth)],
            piece(i, g, half * n, n),
            gsend.at[1],
            grecv.at[0, i],
            {"grp": across},
        )

    def own_across_sixth(i, p):
        r = half * share[1] + p
        return remote(
            source(i).at[rows(r * sixth, sixth, sixth)], piece(i, g, r, 1), gsend.at[1], grecv.at[0, i], {"grp": across}
        )

    def own_over(i):
        return remote(
            source(i).at[rows((4 + half) * sixth, sixth, sixth)],
            stage(0, i),
            gsend.at[5],
            grecv.at[2, i],
            {"section": 1 - s},
        )

    def y_part(i, n):
        return piece(i, far, half * n, n)

    def z_part(i, n):
        return piece(i, far, (1 - half) * n, n)

    def y_to_z(i, n):
        return remote(y_part(i, n), y_part(i, n), gsend.at[2], grecv.at[1, i], {"dp": zpair})

    def y_to_twin(i, n):
        return remote(y_part(i, n), y_part(i, n), gsend.at[3], nrecv.at[1, group_of(i)], {"grp": twin})

    def z_to_twin(i, n):
        return remote(z_part(i, n), z_part(i, n), gsend.at[4], nrecv.at[2, group_of(i)], {"grp": twin})

    def over_to_twin(i):
        both = piece(i, far, 4, 2)
        return remote(both, both, gsend.at[6], nrecv.at[3, group_of(i)], {"grp": twin})

    def wait_for(ref, sem):
        remote(ref, ref, gsend.at[0], sem, {"grp": twin}).wait_recv()

    def stage_across(i):
        return remote(stage(0, i), stage(1, i), gsend.at[5], grecv.at[3, i], {"grp": across})

    def stage_to_z(i):
        return remote(stage(1, i), stage(2, i), gsend.at[7], grecv.at[4, i], {"dp": zpair})

    def stage_back(k, i):
        which = half if k == 1 else 1 - half
        return remote(stage(k, i), piece(i, far, 4 + which, 1), gsend.at[6], grecv.at[2, i], {"section": 1 - s})

    def bulk(n, send, recv, peer):
        return remote(w.at[pl.ds(0, n)], w.at[pl.ds(0, n)], send, recv, peer)

    def near_ready(k):
        n = group_size[k] * quarter
        bulk(n, gsend.at[0], nrecv.at[0, k], {"grp": twin}).wait_recv()
        pltpu.make_async_copy(w.at[pl.ds(0, n)], w.at[pl.ds(0, n)], own_sem.at[k]).wait()

    def far_ready(k, section):
        n = group_size[k] * share[section] * sixth
        bulk(n, gsend.at[3], nrecv.at[1, k], {"grp": twin}).wait_recv()
        bulk(n, gsend.at[4], nrecv.at[2, k], {"grp": twin}).wait_recv()
        if section == 0:
            bulk(group_size[k] * 2 * sixth, gsend.at[6], nrecv.at[3, k], {"grp": twin}).wait_recv()

    def all_ready(k, section):
        near_ready(k)
        far_ready(k, section)

    def gather_order(k):
        return jnp.where(k < 3, QKV0 + k, jnp.where(k == 3, PROJ, jnp.where(k < 8, k, k - 8)))

    def when_block(k, body):
        pl.when(jnp.logical_and(k >= 0, k < CHUNKS))(lambda: body(gather_order(k)))

    zlag, overlag = 2, 5
    ylag, backlag = 2, 4

    def pass_on(k, section):
        n = share[section]

        def from_y(i):
            wait_for(y_part(i, n), grecv.at[0, i])
            y_to_z(i, n).start()
            y_to_twin(i, n).start()

        def from_z(i):
            wait_for(z_part(i, n), grecv.at[1, i])
            z_to_twin(i, n).start()

        when_block(k, from_y)
        when_block(k - zlag, from_z)

    def gather_step(k):
        def from_over(i):
            wait_for(piece(i, far, 4, 2), grecv.at[2, i])
            over_to_twin(i).start()

        pass_on(k, 0)
        when_block(k - overlag, from_over)

    def second_step(k):
        pass_on(k, 1)

    early_blocks = 1 + CHUNKS // share[1]

    def start_sixth(k):
        for m, i in enumerate(GATHER_ORDER[:early_blocks]):
            pl.when(k // share[1] == m)(lambda: own_across_sixth(i, lax.rem(k, share[1])).start())

    def help_step(k):
        def from_x(i):
            wait_for(stage(0, i), grecv.at[2, i])
            stage_across(i).start()

        def from_y(i):
            wait_for(stage(1, i), grecv.at[3, i])
            stage_back(1, i).start()
            stage_to_z(i).start()

        def from_z(i):
            wait_for(stage(2, i), grecv.at[4, i])
            stage_back(2, i).start()

        when_block(k, from_x)
        when_block(k - ylag, from_y)
        when_block(k - backlag, from_z)

    def load(src, dst, k):
        return pltpu.make_async_copy(src, dst, in_sem.at[k])

    table_copy = load(table_hbm, dpk.at[pl.ds(0, table_rows)], 0)
    emb_copy = load(emb_hbm, outb, 1)

    def cot_copy(mb):
        return load(cot_hbm.at[mb], glow.at[rows(mb * seq, seq, seq)], 2 + mb)

    @pl.when(x0)
    def _():
        table_copy.start()
        emb_copy.start()

    @pl.when(x1)
    def _():
        for mb in range(2):
            cot_copy(mb).start()

    for i in GATHER_ORDER:
        own_copy(i).start()
    sums[...] = jnp.zeros_like(sums)
    for mb in range(2):
        maskc[mb] = jnp.transpose(jnp.broadcast_to(mask_ref[mb : mb + 1, :].astype(F32), (128, seq)))

    def enter():
        pl.semaphore_wait(barrier, len(peers))

    enter()

    def issue():
        @pl.when(x0)
        def _():
            for i in GATHER_ORDER:
                own_across(i, share[0]).start()
                own_over(i).start()

        @pl.when(x1)
        def _():
            own_across(GATHER_ORDER[0], share[1]).start()

        for i in GATHER_ORDER:
            own_to_twin(i).start()

    issue()

    def chunk(k):
        return w[rows(k * width, width, width), :]

    step_rows = 32
    parts_of = seq // step_rows
    lane = lax.broadcasted_iota(jnp.int32, (1, 128), 1)
    low_lane = lax.broadcasted_iota(jnp.int32, (seq, 128), 1) < HEAD
    low_half = (lane < HEAD).astype(F32)
    masks = (low_half.astype(BF), (1.0 - low_half).astype(BF))
    scaled = ((low_half * 0.125).astype(BF), ((1.0 - low_half) * 0.125).astype(BF))

    def seq_rows(mb):
        return rows(mb * seq, seq, seq)

    def sub_rows(mb, r):
        return rows(mb * seq + r * step_rows, step_rows, step_rows)

    def r_rows(r):
        return rows(r * step_rows, step_rows, step_rows)

    def norm_parts(v):
        center = v - jnp.mean(v, axis=-1, keepdims=True)
        spread = jnp.mean(center * center, axis=-1, keepdims=True)
        inv = lax.rsqrt(spread + EPS)
        return center * inv, inv

    @pl.when(x1)
    def _():
        def help_and_gather(k):
            help_step(k)
            pl.when(k < CHUNKS)(lambda: start_sixth(k + share[1]))
            pl.when(lax.rem(k, 3) == 1)(lambda: second_step(k // 3))

        loop(CHUNKS, help_and_gather)
        for i in GATHER_ORDER[early_blocks:]:
            own_across(i, share[1]).start()
        loop(CHUNKS + backlag, help_and_gather, CHUNKS)
        loop(11, second_step, early_blocks)
        all_ready(3, 1)
        all_ready(2, 1)

    @pl.when(x0)
    def _():
        table_copy.wait()
        emb_copy.wait()
        ids = lax.broadcasted_iota(jnp.int32, (8, table_rows), 1)
        pick = lax.broadcasted_iota(jnp.int32, (8, table_rows), 0)
        want = jnp.where(pick == 0, times_ref[0], times_ref[1])
        hot = jnp.where(jnp.logical_and(pick < 2, ids == want), 1.0, 0.0).astype(BF)
        trow[...] = dot_nn(hot, dpk[pl.ds(0, table_rows), :])
        vector = vector_ref[...].astype(F32).reshape(1, width)
        for mb in range(2):

            def make(r):
                m = maskc[mb, r_rows(r), 0:1]
                base = jnp.where(m > 0.5, vector, outb[mb, r_rows(r), :].astype(F32))
                h[mb, r_rows(r), :] = base + trow[mb : mb + 1, :]

            loop(parts_of, make)

    def more(mb, t, k):
        @pl.when(x0)
        def _():
            if k < 2:
                gather_step(8 + 2 * t + k)
            else:
                pl.when(t == 1)(lambda: gather_step(12))

        if k < 2:
            pl.when(jnp.logical_and(x1, t == 0))(lambda: second_step(11 + k))

    def first_half(mb, t):
        @pl.when(x1)
        def _():
            h[mb] = relay[mb].astype(F32)

        def ln(r):
            xhat, _ = norm_parts(h[mb, r_rows(r), :])
            normed[sub_rows(mb, r), :] = (xhat * gains_ref[0:1, :]).astype(BF)

        unrolled(parts_of, ln)

        @pl.when(jnp.logical_and(x0, t == 0))
        def _():
            loop(8, gather_step)
            all_ready(3, 0)

        def qkv(k):
            packed[k, seq_rows(mb), :] = dot_nn(normed[seq_rows(mb), :], chunk(QKV0 + k)).astype(BF)

        loop(3, qkv)

        more(mb, t, 0)

        def attend(j):
            cols = pl.ds(j * 128, 128)
            q2 = packed[0, seq_rows(mb), cols]
            k2 = packed[1, seq_rows(mb), cols]
            v2 = packed[2, seq_rows(mb), cols]
            got = []
            for e in range(2):
                sc = dot_nt(q2 * scaled[e], k2)
                ex = jnp.exp(sc - jnp.max(sc, axis=-1, keepdims=True)).astype(BF)
                probs[mb, 2 * j + e] = ex
                got.append(dot_nn(ex, v2 * masks[e] + masks[1 - e]))
            inv = 1.0 / pltpu.roll(jnp.where(low_lane, got[1], got[0]), HEAD, 1)
            inv_sum[mb, :, cols] = inv
            mixed[seq_rows(mb), cols] = (jnp.where(low_lane, got[0], got[1]) * inv).astype(BF)

        unrolled(HEADS // 2, attend)

        more(mb, t, 1)

        pl.when(jnp.logical_and(x0, t == 0))(lambda: all_ready(2, 0))
        mid[mb] = h[mb] + dot_nn(mixed[seq_rows(mb), :], chunk(PROJ))

        def ln_two(r):
            xhat, _ = norm_parts(mid[mb, r_rows(r), :])
            n2[sub_rows(mb, r), :] = (xhat * gains_ref[1:2, :]).astype(BF)

        unrolled(parts_of, ln_two)
        more(mb, t, 2)

    def mlp_up(q, mb):
        lhs = n2[seq_rows(mb), :]
        piece = 256
        chunk_rows = rows((IN0 + q) * width, width, width)

        def product(j):
            return dot_nn(lhs, w[chunk_rows, pl.ds(j * piece, piece)])

        up = product(0)
        for j in range(width // piece):
            after = product(j + 1) if (j + 1) * piece < width else None
            cols = pl.ds(j * piece, piece)
            sq = up * up
            hp = 0.5 + 0.5 * jnp.tanh(up * (GELU_C + (GELU_C * 0.044715) * sq))
            act = up * hp
            actv[q, seq_rows(mb), cols] = act.astype(BF)
            gp[q, seq_rows(mb), cols] = (
                hp + act * ((1.0 - hp) * (2.0 * GELU_C + (2.0 * GELU_C * 0.134145) * sq))
            ).astype(BF)
            up = after

    def mlp_down(q, mb):
        acc[mb] += dot_nn(actv[q, seq_rows(mb), :], chunk(OUT0 + q))

    def second_half_one(mb, t):
        def at_first(body):
            pl.when(t == 0)(body)

        at_first(lambda: all_ready(1, 1))
        for q in range(4):
            mlp_up(q, mb)
        acc[mb] = mid[mb]
        at_first(lambda: near_ready(0))
        for r in range(2):
            mlp_down(2 * y + r, mb)

        @at_first
        def _():
            second_step(13)
            far_ready(0, 1)
            for k, n in ((5, 1), (6, 2), (7, 1)):
                bulk(CHUNKS * n * sixth, gsend.at[k], grecv.at[0, 0], {"grp": twin}).wait_send()

        for r in range(2):
            mlp_down(2 * (1 - y) + r, mb)
        outb[mb] = acc[mb].astype(BF)

    def second_half_both():
        all_ready(1, 0)

        def up(i):
            q, mb = i // 2, lax.rem(i, 2)
            mlp_up(q, mb)

            pl.when(lax.rem(i, 2) == 1)(lambda: gather_step(13 + i // 2))

        loop(8, up)
        acc[...] = mid[...]
        near_ready(0)
        loop(4, lambda i: mlp_down(2 * y + i // 2, lax.rem(i, 2)))
        far_ready(0, 0)

        def down(mb):
            for r in range(2):
                mlp_down(2 * (1 - y) + r, mb)
            outb[mb] = acc[mb].astype(BF)
            relay_copy(mb, 0).start()
            relay_copy(mb, 1).start()
            act_copy(mb).start()

        loop(2, down)

    def relay_copy(mb, part):
        r = pl.ds(part * (seq // 2), seq // 2)
        return remote(
            outb.at[mb, r], relay.at[mb, r], rsend.at[mb, part], rrecv.at[mb, part], {"section": 1 - s}
        )

    def act_copy(mb):
        return pltpu.make_async_copy(outb.at[mb], act_out.at[mb], osem.at[0, mb])

    def dx_copy(mb):
        return pltpu.make_async_copy(h.at[mb], dx_out.at[mb], osem.at[1, mb])

    def norm_back(v, gain, dy):
        xhat, inv = norm_parts(v)
        dxh = dy * gain
        m1 = jnp.mean(dxh, axis=-1, keepdims=True)
        m2 = jnp.mean(dxh * xhat, axis=-1, keepdims=True)
        return inv * (dxh - m1 - xhat * m2), jnp.sum(dy * xhat, axis=0, keepdims=True)

    def backward_mlp(mb, t):
        @pl.when(x0)
        def _():
            glow[seq_rows(mb), :] = relay[mb]

        @pl.when(x1)
        def _():
            cot_copy(mb).wait()

        tmp[...] = jnp.zeros_like(tmp)

        def slope(q):
            da = dot_nt(glow[seq_rows(mb), :], chunk(OUT0 + q))
            du = (gp[q, seq_rows(mb), :].astype(F32) * da).astype(BF)
            gp[q, seq_rows(mb), :] = du
            return du

        def back_up(q):
            tmp[...] += dot_nt(gp[q, seq_rows(mb), :], chunk(IN0 + q))

        def mlp(q):
            tmp[...] += dot_nt(slope(q), chunk(IN0 + q))

        def slope_and_out(k):
            slope(out_order(k))
            out_terms(k)

        last = jnp.logical_and(x0, t == 3)

        @pl.when(last)
        def _():
            loop(4, slope_and_out)
            loop(4, back_up)

        pl.when(jnp.logical_not(last))(lambda: loop(4, mlp))

        def ln_two(r):
            dx, dg = norm_back(mid[mb, r_rows(r), :], gains_ref[1:2, :], tmp[r_rows(r), :])
            dm = glow[sub_rows(mb, r), :].astype(F32) + dx
            mid[mb, r_rows(r), :] = dm
            dmlow[sub_rows(mb, r), :] = dm.astype(BF)
            sums[1:2, :] += dg

        unrolled(parts_of, ln_two)

    def backward_attention(mb, t):
        do_ref[...] = (dot_nt(dmlow[seq_rows(mb), :], chunk(PROJ)) * inv_sum[mb]).astype(BF)

        def attend(j):
            cols = pl.ds(j * 128, 128)
            q2 = packed[0, seq_rows(mb), cols]
            k2 = packed[1, seq_rows(mb), cols]
            v2 = packed[2, seq_rows(mb), cols]
            do2 = do_ref[:, cols]
            weighed = do2.astype(F32) * mixed[seq_rows(mb), cols].astype(F32)
            dq = jnp.zeros((seq, 128), F32)
            dk = jnp.zeros((seq, 128), F32)
            dv = jnp.zeros((seq, 128), F32)
            for e in range(2):
                ex = probs[mb, 2 * j + e]
                dom = do2 * masks[e]
                inner = jnp.sum(jnp.where(low_lane if e == 0 else jnp.logical_not(low_lane), weighed, 0.0), axis=-1, keepdims=True)
                ds = (ex.astype(F32) * (dot_nt(dom, v2) - inner)).astype(BF)
                dv = dv + dot_tn(ex, dom)
                dq = dq + dot_nn(ds, k2 * scaled[e])
                dk = dk + dot_tn(ds, q2 * scaled[e])
            for k, v in enumerate((dq, dk, dv)):
                dpk[rows(k * 2 * seq + mb * seq, seq, seq), cols] = v.astype(BF)

        for j in range(HEADS // 2):
            attend(j)

        early_tick(t, 5)
        early_tick(t, 6)
        tmp[...] = jnp.zeros_like(tmp)

        def qkv(k):
            tmp[...] += dot_nt(dpk[rows(k * 2 * seq + mb * seq, seq, seq), :], chunk(QKV0 + k))

        loop(3, qkv)
        early_tick(t, 7)
        act_copy(mb).wait()

        @pl.when(x0)
        def _():
            for part in range(2):
                relay_copy(mb, part).wait_send()

        for part in range(2):

            def ln_one(rr):
                r = rr + part * (parts_of // 2)
                dx, dg = norm_back(h[mb, r_rows(r), :], gains_ref[0:1, :], tmp[r_rows(r), :])
                dm = mid[mb, r_rows(r), :] + dx
                outb[mb, r_rows(r), :] = dm.astype(BF)
                sums[0:1, :] += dg
                m = maskc[mb, r_rows(r), 0:1]
                kept = jnp.where(jnp.logical_and(x0, m > 0.5), 0.0, dm)
                h[mb, r_rows(r), :] = kept
                sums[pl.ds(2 + mb, 1), :] += jnp.sum(dm, axis=0, keepdims=True)
                sums[4:5, :] += jnp.sum(dm - kept, axis=0, keepdims=True)

            unrolled(parts_of // 2, ln_one)

            @pl.when(x1)
            def _():
                relay_copy(mb, part).start()

        dx_copy(mb).start()
        early_tick(t, 8)

    def grad_chunk(a, b, k):
        w[rows(k * width, width, width), :] = dot_tn(a, b).astype(BF)

    def cslot(i, yy):
        return cbuf.at[yy, rows(i * quarter, quarter, quarter)]

    def to_twin(i, yy):
        q = 2 * yy + (1 - c)
        return remote(
            w.at[rows(place(i, q), quarter, quarter)], cslot(i, yy), csend.at[yy], crecv.at[yy, i // 4], {"grp": twin}
        )

    def from_twin(k, yy):
        ref = cbuf.at[yy, rows(4 * k * quarter, 4 * quarter, quarter)]
        remote(ref, ref, csend.at[yy], crecv.at[yy, k], {"grp": twin}).wait_recv()

    def urows(u):
        return rows(u * unit, unit, unit)

    def y_send(u):
        k = lax.rem(u, YRING)
        return remote(
            cbuf.at[1 - y, urows(u)], ybuf.at[urows(u)], ysend.at[k], yrecv.at[k], {"grp": across}
        )

    def merge_far(i):
        pl.when(lax.rem(i, 4) == 0)(lambda: from_twin(i // 4, 1 - y))
        part = rows(i * quarter, quarter, quarter)
        mine = w[rows(place(i, 2 * (1 - y) + c), quarter, quarter), :].astype(F32)
        cbuf[1 - y, part, :] = (cbuf[1 - y, part, :].astype(F32) + mine).astype(BF)

    ahead = 6

    def send_across(u):
        pl.when(lax.rem(u, per_block) == 0)(lambda: merge_far(u // per_block))
        pl.when(u >= YRING)(lambda: y_send(u - YRING).wait_send())
        y_send(u).start()

    def out_order(k):
        side = jnp.where(k < 2, 1 - y, y)
        return 2 * side + jnp.where(lax.rem(k, 2) == 0, 1 - c, c)

    def out_terms(k):
        q = out_order(k)
        grad_chunk(actv[q], glow[...], OUT0 + q)

        @pl.when(lax.rem(k, 2) == 0)
        def _():
            loop(4, lambda i: to_twin(i, jnp.where(k == 0, 1 - y, y)).start())

        @pl.when(k == 1)
        def _():
            loop(ahead, send_across)

    def other_terms(i, a, b):
        grad_chunk(a, b, i)
        to_twin(i, 1 - y).start()
        to_twin(i, y).start()

    def in_terms():
        early_tick_now(0)

        def one(q):
            other_terms(IN0 + q, n2[...], gp[q])
            early_tick_now(1 + q)

        loop(4, one)

    def attention_terms():
        first = jnp.where(x0, 9, 5)
        other_terms(PROJ, mixed[...], dmlow[...])
        early_tick_now(first)

        def one(k):
            other_terms(QKV0 + k, normed[...], dpk[rows(k * 2 * seq, 2 * seq, 2 * seq), :])
            early_tick_now(first + 1 + k)

        loop(3, one)

    def add_rows(dst, dst_rows, *terms):
        dst[dst_rows, :] = functools.reduce(jnp.add, [a.astype(F32) for a in terms]).astype(BF)

    def sum_across(u):
        i = u // per_block
        pl.when(lax.rem(u, 4 * per_block) == 0)(lambda: from_twin(i // 4, y))
        y_send(u).wait_recv()
        mine = w[rows(place(i, g) + lax.rem(u, per_block) * unit, unit, unit), :]
        add_rows(ybuf, urows(u), cbuf[y, urows(u), :], mine, ybuf[urows(u), :])

    first_tick = jnp.where(x0, 13, 9)
    if nz == 4:
        end = jnp.logical_or(d == 0, d == 3)
        inner = jnp.logical_not(end)
        slots, landed = extra
        pay_copy = remote(pay, landed.at[0], psend.at[0], precv.at[0], {"section": 1 - s})
        last_part = pl.ds(8, 8)

        sums_rows = pl.ds(nz * 8, 8)

        def small_copy(k):
            peer = ({"grp": twin}, {"grp": across}, {"dp": zpair}, {"dp": zfar})[k]
            part = pl.ds(0, 16) if k < 3 else last_part
            return remote(pay.at[part], landed.at[1 + k, part], psend.at[1 + k], precv.at[1 + k], peer)

        pair_rows = rows((d // 2) * 16, 16, 16)
        far_rows = rows((1 - d // 2) * 16, 16, 16)
        pair_copy = remote(slots.at[pair_rows], slots.at[pair_rows], psend.at[5], precv.at[5], {"dp": zfar})
        pair_wait = remote(slots.at[far_rows], slots.at[far_rows], psend.at[5], precv.at[5], {"dp": zfar})
        give_back = remote(slots, slots, psend.at[6], precv.at[6], {"section": 1 - s})

        def small_start():
            pay_copy.wait_recv()
            pay[0:8, :] = landed[0, 0:8, :]
            row = lax.broadcasted_iota(jnp.int32, (8, width + 128), 0)
            other = landed[0, last_part, :]
            pay[last_part, :] = jnp.where(
                row < 2, pay[last_part, :], jnp.where(row == 2, other, pltpu.roll(other, 3, 0))
            )
            small_copy(0).start()

        def small_next(k):
            small_copy(k).wait_recv()
            small_copy(k).wait_send()
            if k < 2:
                pay[...] = pay[...] + landed[1 + k]
                if k == 1:
                    slots[rows(d * 8, 8, 8), :] = pay[0:8, :]
                small_copy(k + 1).start()
            else:
                slots[rows(zpair * 8, 8, 8), :] = landed[3, 0:8, :]
                pay[last_part, :] = pay[last_part, :] + landed[3, last_part, :]
                small_copy(3).start()
                pair_copy.start()

        def small_end():
            small_copy(3).wait_recv()
            small_copy(3).wait_send()
            pair_wait.wait_recv()
            slots[sums_rows, :] = pay[last_part, :] + landed[4, last_part, :]
            give_back.start()

        def small_results():
            pl.when(x0)(lambda: give_back.wait_recv())
            total = slots[sums_rows, 0:width]
            shard = s * 4 + g
            mine = jnp.where(x0, pltpu.roll(total, 5, 0), total)
            small_out[0:8, :] = pltpu.roll(mine, lax.rem(width - quarter * g, width), 1)
            small_out[8:16, :] = pltpu.roll(total, lax.rem(width - (width // 8) * shard, width), 1)
            base = shard * (table_rows // 8) + 1
            ids = (base + lax.broadcasted_iota(jnp.int32, (nz * 8, 128), 1)).astype(F32)
            pick = jnp.where(slots[0 : nz * 8, pl.ds(width, 128)] == ids, 1.0, 0.0).astype(BF)
            rest = slots[0 : nz * 8, 0:width]
            found = jnp.zeros((128, width), F32)
            for _ in range(3):
                part = rest.astype(BF)
                found = found + dot_tn(pick, part)
                rest = rest - part.astype(F32)
            table_out[...] = found

        def zcopy(src, dst, k, u, peer):
            m = lax.rem(u, ZRING)
            return remote(src.at[urows(u)], dst.at[urows(u)], zsend.at[k, m], zrecv.at[k, m], peer)

        def end_to_inner(u):
            return zcopy(ybuf, z1, 0, u, {"dp": zpair})

        def inner_swap(u):
            return zcopy(z1, z2, 1, u, {"dp": 3 - d})

        def inner_to_end(u):
            return zcopy(z2, z1, 0, u, {"dp": zpair})

        def grad_copy(src, u):
            return pltpu.make_async_copy(src.at[urows(u)], grad_out.at[urows(u)], zout.at[lax.rem(u, ZRING)])

        def launch(copy, u):
            pl.when(u >= ZRING)(lambda: copy(u - ZRING).wait_send())
            copy(u).start()

        def put_out(src, u):
            pl.when(u >= ZRING)(lambda: grad_copy(src, u - ZRING).wait())
            grad_copy(src, u).start()

        lag3, lag4, lag5 = 3, 6, 9
        first_small, small_gap = 16, 6

        def tick(t, small=True):
            u2, u3, u4, u5 = t, t - lag3, t - lag4, t - lag5
            pl.when(u2 + ahead < units)(lambda: send_across(u2 + ahead))

            @pl.when(u2 < units)
            def _():
                sum_across(u2)

                @pl.when(end)
                def _():
                    launch(end_to_inner, u2)

            @pl.when(jnp.logical_and(inner, jnp.logical_and(u3 >= 0, u3 < units)))
            def _():
                end_to_inner(u3).wait_recv()
                add_rows(z1, urows(u3), ybuf[urows(u3), :], z1[urows(u3), :])
                launch(inner_swap, u3)

            @pl.when(jnp.logical_and(inner, jnp.logical_and(u4 >= 0, u4 < units)))
            def _():
                inner_swap(u4).wait_recv()
                add_rows(z2, urows(u4), z1[urows(u4), :], z2[urows(u4), :])
                launch(inner_to_end, u4)
                put_out(z2, u4)

            @pl.when(jnp.logical_and(end, jnp.logical_and(u5 >= 0, u5 < units)))
            def _():
                inner_to_end(u5).wait_recv()
                put_out(z1, u5)

            if not small:
                return
            pl.when(t == jnp.where(x1, units, units + 2))(small_results)

            @pl.when(x1)
            def _():
                pl.when(t == first_small)(small_start)
                for k in range(3):
                    pl.when(t == first_small + small_gap * (k + 1))(functools.partial(small_next, k))
                pl.when(t == first_small + small_gap * 4)(small_end)

    else:

        def out_sum(u):
            return pltpu.make_async_copy(ybuf.at[urows(u)], grad_out.at[urows(u)], zout.at[lax.rem(u, ZRING)])

        def tick(u, small=True):
            pl.when(u + ahead < units)(lambda: send_across(u + ahead))
            sum_across(u)
            pl.when(u >= ZRING)(lambda: out_sum(u - ZRING).wait())
            out_sum(u).start()

    def early_tick_now(t):
        tick(t, False)

    def early_tick(t, k):
        pl.when(jnp.logical_and(x0, t == 3))(lambda: early_tick_now(k))

    def step(t):
        mb = jnp.where(x0, lax.rem(t, 2), t // 2)
        is_f = jnp.where(x0, t < 2, lax.rem(t, 2) == 0)

        @pl.when(is_f)
        def _():
            @pl.when(x1)
            def _():
                relay_copy(mb, 0).wait_recv()
                relay_copy(mb, 1).wait_recv()

            first_half(mb, t)

            pl.when(jnp.logical_and(x0, t == 1))(second_half_both)

            @pl.when(x1)
            def _():
                second_half_one(mb, t)
                act_copy(mb).start()

        @pl.when(jnp.logical_not(is_f))
        def _():
            @pl.when(x0)
            def _():
                for part in range(2):
                    relay_copy(mb, part).wait_recv()

            @pl.when(jnp.logical_and(x0, t == 3))
            def _():
                gather_sent(0)

            backward_mlp(mb, t)

            @pl.when(jnp.logical_and(x0, t == 3))
            def _():
                in_terms()

            backward_attention(mb, t)

    def gather_sent(section):
        bulk(CHUNKS * quarter, gsend.at[0], nrecv.at[0, 0], {"grp": twin}).wait_send()
        n = CHUNKS * share[section] * sixth
        for k in range(1, 5):
            bulk(n, gsend.at[k], grecv.at[0, 0], {"grp": twin}).wait_send()
        if section == 0:
            for k, n in ((5, 1), (6, 2)):
                bulk(CHUNKS * n * sixth, gsend.at[k], grecv.at[0, 0], {"grp": twin}).wait_send()

    loop(4, step)

    @pl.when(x1)
    def _():
        gather_sent(1)
        loop(4, out_terms)
        in_terms()

    row_ids = lax.broadcasted_iota(jnp.int32, (8, width), 0)
    stamp_ids = lax.broadcasted_iota(jnp.int32, (8, 128), 0)
    first = 2 * g
    pay[0:8, 0:width] = jnp.where(
        row_ids == first, sums[2:3, :], jnp.where(row_ids == first + 1, sums[3:4, :], 0.0)
    )
    pay[0:8, pl.ds(width, 128)] = jnp.where(
        stamp_ids == first,
        (times_ref[0] + 1).astype(F32),
        jnp.where(stamp_ids == first + 1, (times_ref[1] + 1).astype(F32), 0.0),
    )
    pay[8:16, 0:width] = jnp.where(
        row_ids < 2, sums[...], jnp.where(row_ids == 2, sums[4:5, :], 0.0)
    )
    pay[8:16, pl.ds(width, 128)] = jnp.zeros((8, 128), F32)

    if nz == 4:
        pl.when(x0)(lambda: pay_copy.start())

    attention_terms()

    if nz == 4:
        loop(units + lag5, tick, first_tick)

        loop(units, lambda u: y_send(u).wait_send(), units - YRING)

        def drain(u):
            @pl.when(end)
            def _():
                end_to_inner(u).wait_send()
                grad_copy(z1, u).wait()

            @pl.when(inner)
            def _():
                inner_swap(u).wait_send()
                inner_to_end(u).wait_send()
                grad_copy(z2, u).wait()

        loop(units, drain, units - ZRING)

        pl.when(x0)(lambda: pay_copy.wait_send())

        @pl.when(x1)
        def _():
            pair_copy.wait_send()
            give_back.wait_send()

    else:
        small_out[...] = pay[...]
        table_out[...] = jnp.zeros_like(table_out)
        loop(units, tick, first_tick)

        loop(units, lambda u: y_send(u).wait_send(), units - YRING)
        loop(units, lambda u: out_sum(u).wait(), units - ZRING)

    for yy in range(2):
        bulk(CHUNKS * quarter, csend.at[yy], crecv.at[yy, 0], {"grp": twin}).wait_send()

    for mb in range(2):
        dx_copy(mb).wait()

        @pl.when(x1)
        def _():
            for part in range(2):
                relay_copy(mb, part).wait_send()


def run_mega(timesteps, mask_flags, vector, gains, emb, cot, table, wq, wp, wi, wo, nz):
    count, seq, width = emb.shape
    quarter = wp.shape[0]
    unit = quarter // 4
    units = CHUNKS * quarter // unit
    tokens = count * seq
    assert count == 2 and quarter * 4 == width and wi.shape[1] == 4 * width and wo.shape[0] == width
    vmem = pl.BlockSpec(memory_space=pltpu.VMEM)
    smem = pl.BlockSpec(memory_space=pltpu.SMEM)
    hbm = pl.BlockSpec(memory_space=pl.ANY)
    dma = pltpu.SemaphoreType.DMA
    small = (16, width) if nz == 4 else (16, width + 128)
    extra = [pltpu.VMEM((nz * 8 + 8, width + 128), F32), pltpu.VMEM((5, 16, width + 128), F32)]
    return pl.pallas_call(
        functools.partial(mega, (count, seq, width, nz, unit)),
        out_shape=(
            jax.ShapeDtypeStruct((count, seq, width), BF),
            jax.ShapeDtypeStruct((count, seq, width), F32),
            jax.ShapeDtypeStruct((CHUNKS * quarter, width), BF),
            jax.ShapeDtypeStruct(small, F32),
            jax.ShapeDtypeStruct((128, width), F32),
        ),
        in_specs=[smem, vmem, vmem, vmem] + [hbm] * 7,
        out_specs=(hbm, hbm, hbm, vmem, vmem),
        scratch_shapes=[
            pltpu.VMEM((CHUNKS * width, width), BF),
            pltpu.VMEM((count, seq, width), F32),
            pltpu.VMEM((count, seq, width), F32),
            pltpu.VMEM((count, seq, width), F32),
            pltpu.VMEM((seq, width), F32),
            pltpu.VMEM((count, seq, width), F32),
            pltpu.VMEM((tokens, width), BF),
            pltpu.VMEM((tokens, width), BF),
            pltpu.VMEM((tokens, width), BF),
            pltpu.VMEM((4, tokens, width), BF),
            pltpu.VMEM((4, tokens, width), BF),
            pltpu.VMEM((3, tokens, width), BF),
            pltpu.VMEM((count, HEADS, seq, seq), BF),
            pltpu.VMEM((tokens, width), BF),
            pltpu.VMEM((tokens, width), BF),
            pltpu.VMEM((3 * tokens, width), BF),
            pltpu.VMEM((seq, width), BF),
            pltpu.VMEM((count, seq, width), BF),
            pltpu.VMEM((count, seq, width), BF),
            pltpu.VMEM((count, seq, 128), F32),
            pltpu.VMEM((8, width), F32),
            pltpu.VMEM((16, width + 128), F32),
            pltpu.VMEM((8, width), F32),
            pltpu.VMEM((2, CHUNKS * quarter, width), BF),
            pltpu.VMEM((CHUNKS * quarter, width), BF),
            pltpu.VMEM((CHUNKS * quarter, width), BF),
            pltpu.VMEM((CHUNKS * quarter, width), BF),
            dma((4,)),
            dma((4,)),
            dma((8,)),
            dma((5, CHUNKS)),
            dma((4, 4)),
            dma((2, 2)),
            dma((2, 2)),
            dma((2,)),
            dma((2, 3)),
            dma((YRING,)),
            dma((YRING,)),
            dma((2, ZRING)),
            dma((2, ZRING)),
            dma((ZRING,)),
            dma((7,)),
            dma((7,)),
            dma((2, 2)),
        ]
        + (extra if nz == 4 else []),
        compiler_params=pltpu.CompilerParams(
            collective_id=0, has_side_effects=True, vmem_limit_bytes=67043328
        ),
        name="relay_layers",
    )(timesteps, mask_flags, vector, gains, emb, cot, table, wq, wp, wi, wo)


def place_results(
    act_in,
    dx_in,
    grads_in,
    small_ref,
    table_ref,
    act_out,
    dx_out,
    qkv_out,
    proj_out,
    in_out,
    out_out,
    gains_out,
    table_out,
    mask_out,
    act_buf,
    dx_buf,
    low_buf,
    wide_buf,
    ins,
    outs,
):
    quarter, width = proj_out.shape
    blocks = []
    for i in range(CHUNKS):
        part = pl.ds(i * quarter, quarter)
        if i < IN0:
            target = out_out.at[part]
        elif i < PROJ:
            target = in_out.at[:, pl.ds((i - IN0) * width, width)]
        elif i == PROJ:
            target = proj_out
        else:
            target = qkv_out.at[:, pl.ds((i - QKV0) * width, width)]
        blocks.append(
            (
                part,
                pltpu.make_async_copy(grads_in.at[part], low_buf.at[part], ins.at[i]),
                pltpu.make_async_copy(wide_buf.at[part], target, outs.at[i]),
            )
        )
    plain = [
        (
            pltpu.make_async_copy(dx_in, dx_buf, ins.at[CHUNKS]),
            pltpu.make_async_copy(dx_buf, dx_out, outs.at[CHUNKS]),
        ),
        (
            pltpu.make_async_copy(act_in, act_buf, ins.at[CHUNKS + 1]),
            pltpu.make_async_copy(act_buf, act_out, outs.at[CHUNKS + 1]),
        ),
    ]
    for _, come, _ in blocks:
        come.start()
    for come, _ in plain:
        come.start()
    for part, come, go in blocks:
        come.wait()
        wide_buf[part, :] = low_buf[part, :].astype(F32)
        go.start()
    for come, go in plain:
        come.wait()
        go.start()
    gains_out[...] = small_ref[0:2, 0:quarter]
    table_out[...] = table_ref[0 : table_out.shape[0], :]
    mask_out[...] = small_ref[10, 0 : mask_out.shape[0]]
    for _, _, go in blocks:
        go.wait()
    for _, go in plain:
        go.wait()


def run_place(activations, dx, grads, small, table, quarter, table_here, mask_here):
    count, seq, width = dx.shape
    vmem = pl.BlockSpec(memory_space=pltpu.VMEM)
    hbm = pl.BlockSpec(memory_space=pl.ANY)
    dma = pltpu.SemaphoreType.DMA
    shapes = (
        ((count, seq, width), BF),
        ((count, seq, width), F32),
        ((quarter, 3 * width), F32),
        ((quarter, width), F32),
        ((quarter, 4 * width), F32),
        ((width, width), F32),
        ((2, quarter), F32),
        ((table_here, width), F32),
        ((mask_here,), F32),
    )
    return pl.pallas_call(
        place_results,
        out_shape=tuple(jax.ShapeDtypeStruct(a, b) for a, b in shapes),
        in_specs=[hbm] * 3 + [vmem] * 2,
        out_specs=(hbm,) * 6 + (vmem,) * 3,
        scratch_shapes=[
            pltpu.VMEM((count, seq, width), BF),
            pltpu.VMEM((count, seq, width), F32),
            pltpu.VMEM((CHUNKS * quarter, width), BF),
            pltpu.VMEM((CHUNKS * quarter, width), F32),
            dma((CHUNKS + 2,)),
            dma((CHUNKS + 2,)),
        ],
        compiler_params=pltpu.CompilerParams(vmem_limit_bytes=64000000),
        name="place_results",
    )(activations, dx, grads, small, table)


def small_sums(sizes, small, timesteps, rows_count, quarter):
    ns, ng, nz = sizes
    width = quarter * 4
    section, member = lax.axis_index("section"), lax.axis_index("grp")
    every = lax.all_gather(small, ("section", "grp", "dp"), axis=0, tiled=False)
    per_plane = every.reshape(ns, ng * nz, 16, width + 128)
    mine = lax.dynamic_index_in_dim(per_plane, section, 0, keepdims=False)[:, 8:10, :width].sum(axis=0)
    grad_gains = lax.dynamic_slice(mine, (0, member * quarter), (2, quarter))
    shard = section * ng + member
    here = rows_count // (ns * ng)
    ids = (shard * here + 1 + jnp.arange(here)).astype(F32)
    stamp = per_plane[0, :, :8, width].reshape(-1)
    pick = (ids[:, None] == stamp[None, :]).astype(F32)
    tokens = per_plane[0, :, :8, :width].reshape(-1, width)
    grad_table = jnp.dot(pick, tokens, precision=lax.Precision.HIGHEST)
    mask_here = width // (ns * ng)
    grad_mask = lax.dynamic_slice(per_plane[0, :, 10, :width].sum(axis=0), (shard * mask_here,), (mask_here,))
    return grad_gains, grad_table, grad_mask


def on_device(
    sizes,
    embeddings,
    mask_flags,
    timesteps,
    time_table,
    mask_vector,
    attn_qkv,
    attn_out,
    mlp_in,
    mlp_out,
    norm_gains,
    cotangent,
):
    ns, ng, nz = sizes
    rows_count, width = time_table.shape
    activations, dx, grads, small, table = run_mega(
        timesteps,
        mask_flags,
        mask_vector,
        norm_gains[0],
        embeddings,
        cotangent,
        time_table,
        attn_qkv[0],
        attn_out[0],
        mlp_in[0],
        mlp_out[0],
        nz,
    )
    quarter = attn_out.shape[1]
    table_here, mask_here = rows_count // (ns * ng), width // (ns * ng)
    if nz != 4:
        grads = lax.psum(grads, "dp")
        gain_sums, table_sums, mask_sums = small_sums(sizes, small, timesteps, rows_count, quarter)
    placed = run_place(
        activations, dx, grads, small, table, quarter, table_here, mask_here
    )
    if nz != 4:
        placed = placed[:6] + (gain_sums, table_sums, mask_sums)
    return tuple(v[None] for v in placed[:7]) + placed[7:]


def solution(mesh):
    sizes = (mesh.shape["section"], mesh.shape["grp"], mesh.shape["dp"])
    placed = (
        P(("grp", "dp"), None, None),
        P(("grp", "dp"), None),
        P(("grp", "dp")),
        P(),
        P(),
        P("section", "grp", None),
        P("section", "grp", None),
        P("section", "grp", None),
        P("section", "grp", None),
        P("section", None, None),
        P(("grp", "dp"), None, None),
    )
    return jax.shard_map(
        functools.partial(on_device, sizes),
        mesh=mesh,
        in_specs=placed,
        out_specs=(
            P("section", ("grp", "dp"), None, None),
            P("section", ("grp", "dp"), None, None),
            P("section", "grp", None),
            P("section", "grp", None),
            P("section", "grp", None),
            P("section", "grp", None),
            P("section", None, "grp"),
            P(("section", "grp"), None),
            P(("section", "grp")),
        ),
        check_vma=False,
    )
```

time: 247 us -> 212 us (0.86)
  Pallas kernels: 232 us -> 211 us
  other arithmetic: 6.99 us -> 0 us
  local copies, waits for them, and re-layouts: 6.68 us -> 0 us
    pallas_call x1, Pallas kernels: 232 us -> 203 us  [run_mega(): pl.pallas_call(functools.partial(mega, (count, seq, width, nz, unit)), ou...]
    pallas_call x0 -> x1, Pallas kernels: none -> 7.41 us  [run_place(): pl.pallas_call(place_results, out_shape=tuple((jax.ShapeDtypeStruct(a, b)...]
    broadcast_in_dim x1 -> x0, other arithmetic: 3 us -> none  [on_device(): grads[:4 * quarter].astype(F32)[None]]
    convert_element_type x2 -> x0, other arithmetic: 2.99 us -> none  [blocks(): return jnp.concatenate([grads[(first + j) * quarter:(first + j + 1) * qua...]
    unnamed x11 -> x0, local copies, waits for them, and re-layouts: 2.95 us -> none
    broadcast_in_dim x2 -> x0, local copies, waits for them, and re-layouts: 2.54 us -> none  [the longest x1 1.27 us: on_device(): grad_gains[None]]
where the time goes in v3:
time: 212 us
  Pallas kernels  211 us (100%)
    pallas_call x1, Pallas kernels, run_mega(): pl.pallas_call(functools.partial(mega, (count, seq, width, nz, unit)), ou...  203 us
    pallas_call x1, Pallas kernels, run_place(): pl.pallas_call(place_results, out_shape=tuple((jax.ShapeDtypeStruct(a, b)...  7.41 us

profile of v3, /device:TPU:0, one launch (start us, length us, event | category | flops | bytes accessed | tf_op | source)
XLA Modules:
  0.0 211.6 jit_solution(6987226813027546697)
XLA Ops:
  0.6 203.3 %relay_layers.1 = (bf16[2,256,768]{2,1,0:T(8,128)(2,1)}, f32[2,256,768]{2,1,0:T(8,128)}, bf16[2304,768]{1,0:T(8,128)(2,1)}, f32[16,768]{1,0:T(8,128)}, f32[128,768]{1,0:T(8,128)}) custom-call(s32[2]{0:T(128)} %times_ref.1, s32[2,256]{1,0:T(2,128)} %mask_ref.1, bf16[768]{0:T(1024)(128)(2,1)} %vector_ref.1, f32[2,768]{1,0:T(2,128)} %bitcast.16, ...), custom_call_target="tpu_custom_call" | custom-call | tf_op jit(solution)/shard_map/relay_layers/pallas_call | solution.py:1062
  204.0 7.4 %place_results.1 = (bf16[2,256,768]{2,1,0:T(8,128)(2,1)}, f32[2,256,768]{2,1,0:T(8,128)}, f32[192,2304]{1,0:T(8,128)}, f32[192,768]{1,0:T(8,128)}, f32[192,3072]...) custom-call(bf16[2,256,768]{2,1,0:T(8,128)(2,1)} %get-tuple-element.23.act_in, ...), custom_call_target="tpu_custom_call" | custom-call | tf_op jit(solution)/shard_map/place_results/pallas_call | solution.py:1214

commit v4 on v3

--- a/solution.py
+++ b/solution.py
@@ -58,8 +58,8 @@
     act_out,
     dx_out,
     grad_out,
-    small_out,
-    table_out,
+    small_hbm,
+    table_hbm_out,
     w,
     h,
     mid,
@@ -104,6 +104,8 @@
     psend,
     precv,
     osem,
+    small_out,
+    table_out,
     *extra,
 ):
     count, seq, width, nz, unit = cfg
@@ -444,7 +446,7 @@
         def qkv(k):
             packed[k, seq_rows(mb), :] = dot_nn(normed[seq_rows(mb), :], chunk(QKV0 + k)).astype(BF)
 
-        loop(3, qkv)
+        unrolled(3, qkv)
 
         more(mb, t, 0)
 
@@ -527,27 +529,27 @@
     def second_half_both():
         all_ready(1, 0)
 
-        def up(i):
-            q, mb = i // 2, lax.rem(i, 2)
-            mlp_up(q, mb)
-
-            pl.when(lax.rem(i, 2) == 1)(lambda: gather_step(13 + i // 2))
-
-        loop(8, up)
-        acc[...] = mid[...]
-        near_ready(0)
-        loop(4, lambda i: mlp_down(2 * y + i // 2, lax.rem(i, 2)))
-        far_ready(0, 0)
-
-        def down(mb):
-            for r in range(2):
-                mlp_down(2 * (1 - y) + r, mb)
+        def up(q):
+            mlp_up(q, 0)
+            gather_step(13 + q)
+
+        def finish(mb):
             outb[mb] = acc[mb].astype(BF)
             relay_copy(mb, 0).start()
             relay_copy(mb, 1).start()
             act_copy(mb).start()
 
-        loop(2, down)
+        loop(4, up)
+        acc[...] = mid[...]
+        near_ready(0)
+        loop(2, lambda r: mlp_down(2 * y + r, 0))
+        far_ready(0, 0)
+        loop(2, lambda r: mlp_down(2 * (1 - y) + r, 0))
+        finish(0)
+        for q in range(4):
+            mlp_up(q, 1)
+            mlp_down(q, 1)
+        finish(1)
 
     def relay_copy(mb, part):
         r = pl.ds(part * (seq // 2), seq // 2)
@@ -602,7 +604,7 @@
             loop(4, slope_and_out)
             loop(4, back_up)
 
-        pl.when(jnp.logical_not(last))(lambda: loop(4, mlp))
+        pl.when(jnp.logical_not(last))(lambda: unrolled(4, mlp))
 
         def ln_two(r):
             dx, dg = norm_back(mid[mb, r_rows(r), :], gains_ref[1:2, :], tmp[r_rows(r), :])
@@ -647,7 +649,7 @@
         def qkv(k):
             tmp[...] += dot_nt(dpk[rows(k * 2 * seq + mb * seq, seq, seq), :], chunk(QKV0 + k))
 
-        loop(3, qkv)
+        unrolled(3, qkv)
         early_tick(t, 7)
         act_copy(mb).wait()
 
@@ -688,12 +690,15 @@
     def to_twin(i, yy):
         q = 2 * yy + (1 - c)
         return remote(
-            w.at[rows(place(i, q), quarter, quarter)], cslot(i, yy), csend.at[yy], crecv.at[yy, i // 4], {"grp": twin}
+            w.at[rows(place(i, q), quarter, quarter)], cslot(i, yy), csend.at[yy], crecv.at[arrival(i, yy)], {"grp": twin}
         )
+
+    def arrival(i, yy):
+        return jnp.where(jnp.logical_and(yy == 1 - y, i < IN0), 6 + i, 3 * yy + i // 4)
 
     def from_twin(k, yy):
         ref = cbuf.at[yy, rows(4 * k * quarter, 4 * quarter, quarter)]
-        remote(ref, ref, csend.at[yy], crecv.at[yy, k], {"grp": twin}).wait_recv()
+        remote(ref, ref, csend.at[yy], crecv.at[3 * yy + k], {"grp": twin}).wait_recv()
 
     def urows(u):
         return rows(u * unit, unit, unit)
@@ -705,7 +710,8 @@
         )
 
     def merge_far(i):
-        pl.when(lax.rem(i, 4) == 0)(lambda: from_twin(i // 4, 1 - y))
+        pl.when(i < IN0)(lambda: wait_for(cslot(i, 1 - y), crecv.at[arrival(i, 1 - y)]))
+        pl.when(jnp.logical_and(i >= IN0, lax.rem(i, 4) == 0))(lambda: from_twin(i // 4, 1 - y))
         part = rows(i * quarter, quarter, quarter)
         mine = w[rows(place(i, 2 * (1 - y) + c), quarter, quarter), :].astype(F32)
         cbuf[1 - y, part, :] = (cbuf[1 - y, part, :].astype(F32) + mine).astype(BF)
@@ -837,6 +843,7 @@
                 found = found + dot_tn(pick, part)
                 rest = rest - part.astype(F32)
             table_out[...] = found
+            small_leaves()
 
         def zcopy(src, dst, k, u, peer):
             m = lax.rem(u, ZRING)
@@ -922,6 +929,15 @@
 
     def early_tick(t, k):
         pl.when(jnp.logical_and(x0, t == 3))(lambda: early_tick_now(k))
+
+    leaving = (
+        pltpu.make_async_copy(small_out, small_hbm, osem.at[0, 2]),
+        pltpu.make_async_copy(table_out, table_hbm_out, osem.at[1, 2]),
+    )
+
+    def small_leaves():
+        for copy in leaving:
+            copy.start()
 
     def step(t):
         mb = jnp.where(x0, lax.rem(t, 2), t // 2)
@@ -1029,14 +1045,17 @@
     else:
         small_out[...] = pay[...]
         table_out[...] = jnp.zeros_like(table_out)
+        small_leaves()
         loop(units, tick, first_tick)
 
         loop(units, lambda u: y_send(u).wait_send(), units - YRING)
         loop(units, lambda u: out_sum(u).wait(), units - ZRING)
 
     for yy in range(2):
-        bulk(CHUNKS * quarter, csend.at[yy], crecv.at[yy, 0], {"grp": twin}).wait_send()
-
+        bulk(CHUNKS * quarter, csend.at[yy], crecv.at[0], {"grp": twin}).wait_send()
+
+    for copy in leaving:
+        copy.wait()
     for mb in range(2):
         dx_copy(mb).wait()
 
@@ -1069,7 +1088,7 @@
             jax.ShapeDtypeStruct((128, width), F32),
         ),
         in_specs=[smem, vmem, vmem, vmem] + [hbm] * 7,
-        out_specs=(hbm, hbm, hbm, vmem, vmem),
+        out_specs=(hbm,) * 5,
         scratch_shapes=[
             pltpu.VMEM((CHUNKS * width, width), BF),
             pltpu.VMEM((count, seq, width), F32),
@@ -1106,7 +1125,7 @@
             dma((2, 2)),
             dma((2, 2)),
             dma((2,)),
-            dma((2, 3)),
+            dma((10,)),
             dma((YRING,)),
             dma((YRING,)),
             dma((2, ZRING)),
@@ -1114,7 +1133,9 @@
             dma((ZRING,)),
             dma((7,)),
             dma((7,)),
-            dma((2, 2)),
+            dma((2, 3)),
+            pltpu.VMEM(small, F32),
+            pltpu.VMEM((128, width), F32),
         ]
         + (extra if nz == 4 else []),
         compiler_params=pltpu.CompilerParams(

time: 212 us -> 208 us (0.981)
  Pallas kernels: 211 us -> 207 us
    pallas_call x1, Pallas kernels: 203 us -> 199 us  [run_mega(): pl.pallas_call(functools.partial(mega, (count, seq, width, nz, unit)), ou...]
where the time goes in v4:
time: 208 us
  Pallas kernels  207 us (100%)
    pallas_call x1, Pallas kernels, run_mega(): pl.pallas_call(functools.partial(mega, (count, seq, width, nz, unit)), ou...  199 us
    pallas_call x1, Pallas kernels, run_place(): pl.pallas_call(place_results, out_shape=tuple((jax.ShapeDtypeStruct(a, b)...  7.41 us

profile of v4, /device:TPU:0, one launch (start us, length us, event | category | flops | bytes accessed | tf_op | source)
XLA Modules:
  0.0 207.7 jit_solution(12571887922520884024)
XLA Ops:
  0.6 199.4 %relay_layers.1 = (bf16[2,256,768]{2,1,0:T(8,128)(2,1)}, f32[2,256,768]{2,1,0:T(8,128)}, bf16[2304,768]{1,0:T(8,128)(2,1)}, f32[16,768]{1,0:T(8,128)}, f32[128,768]{1,0:T(8,128)}) custom-call(s32[2]{0:T(128)} %times_ref.1, s32[2,256]{1,0:T(2,128)} %mask_ref.1, bf16[768]{0:T(1024)(128)(2,1)} %vector_ref.1, f32[2,768]{1,0:T(2,128)} %bitcast.16, ...), custom_call_target="tpu_custom_call" | custom-call | tf_op jit(solution)/shard_map/relay_layers/pallas_call | solution.py:1081
  200.1 7.4 %place_results.1 = (bf16[2,256,768]{2,1,0:T(8,128)(2,1)}, f32[2,256,768]{2,1,0:T(8,128)}, f32[192,2304]{1,0:T(8,128)}, f32[192,768]{1,0:T(8,128)}, f32[192,3072]...) custom-call(bf16[2,256,768]{2,1,0:T(8,128)(2,1)} %get-tuple-element.23.act_in, ...), custom_call_target="tpu_custom_call" | custom-call | tf_op jit(solution)/shard_map/place_results/pallas_call | solution.py:1235

commit v5 on v4

--- a/solution.py
+++ b/solution.py
@@ -579,8 +579,6 @@
         def _():
             cot_copy(mb).wait()
 
-        tmp[...] = jnp.zeros_like(tmp)
-
         def slope(q):
             da = dot_nt(glow[seq_rows(mb), :], chunk(OUT0 + q))
             du = (gp[q, seq_rows(mb), :].astype(F32) * da).astype(BF)
@@ -591,7 +589,8 @@
             tmp[...] += dot_nt(gp[q, seq_rows(mb), :], chunk(IN0 + q))
 
         def mlp(q):
-            tmp[...] += dot_nt(slope(q), chunk(IN0 + q))
+            got = dot_nt(slope(q), chunk(IN0 + q))
+            tmp[...] = got if q == 0 else tmp[...] + got
 
         def slope_and_out(k):
             slope(out_order(k))
@@ -601,6 +600,7 @@
 
         @pl.when(last)
         def _():
+            tmp[...] = jnp.zeros_like(tmp)
             loop(4, slope_and_out)
             loop(4, back_up)
 
@@ -644,12 +644,10 @@
 
         early_tick(t, 5)
         early_tick(t, 6)
-        tmp[...] = jnp.zeros_like(tmp)
-
-        def qkv(k):
-            tmp[...] += dot_nt(dpk[rows(k * 2 * seq + mb * seq, seq, seq), :], chunk(QKV0 + k))
-
-        unrolled(3, qkv)
+        tmp[...] = functools.reduce(
+            jnp.add,
+            [dot_nt(dpk[rows(k * 2 * seq + mb * seq, seq, seq), :], chunk(QKV0 + k)) for k in range(3)],
+        )
         early_tick(t, 7)
         act_copy(mb).wait()
 
@@ -1196,16 +1194,16 @@
             pltpu.make_async_copy(act_buf, act_out, outs.at[CHUNKS + 1]),
         ),
     ]
+    for come, _ in plain:
+        come.start()
     for _, come, _ in blocks:
         come.start()
-    for come, _ in plain:
-        come.start()
+    for come, go in plain:
+        come.wait()
+        go.start()
     for part, come, go in blocks:
         come.wait()
         wide_buf[part, :] = low_buf[part, :].astype(F32)
-        go.start()
-    for come, go in plain:
-        come.wait()
         go.start()
     gains_out[...] = small_ref[0:2, 0:quarter]
     table_out[...] = table_ref[0 : table_out.shape[0], :]

time: 208 us -> 207 us (level)
  no operation moved by 1% of the time
where the time goes in v5:
time: 207 us
  Pallas kernels  206 us (100%)
    pallas_call x1, Pallas kernels, run_mega(): pl.pallas_call(functools.partial(mega, (count, seq, width, nz, unit)), ou...  199 us
    pallas_call x1, Pallas kernels, run_place(): pl.pallas_call(place_results, out_shape=tuple((jax.ShapeDtypeStruct(a, b)...  7.04 us

profile of v5, /device:TPU:0, one launch (start us, length us, event | category | flops | bytes accessed | tf_op | source)
XLA Modules:
  0.0 207.2 jit_solution(3441298197628687750)
XLA Ops:
  0.6 199.3 %relay_layers.1 = (bf16[2,256,768]{2,1,0:T(8,128)(2,1)}, f32[2,256,768]{2,1,0:T(8,128)}, bf16[2304,768]{1,0:T(8,128)(2,1)}, f32[16,768]{1,0:T(8,128)}, f32[128,768]{1,0:T(8,128)}) custom-call(s32[2]{0:T(128)} %times_ref.1, s32[2,256]{1,0:T(2,128)} %mask_ref.1, bf16[768]{0:T(1024)(128)(2,1)} %vector_ref.1, f32[2,768]{1,0:T(2,128)} %bitcast.16, ...), custom_call_target="tpu_custom_call" | custom-call | tf_op jit(solution)/shard_map/relay_layers/pallas_call | solution.py:1079
  200.0 7.0 %place_results.1 = (bf16[2,256,768]{2,1,0:T(8,128)(2,1)}, f32[2,256,768]{2,1,0:T(8,128)}, f32[192,2304]{1,0:T(8,128)}, f32[192,768]{1,0:T(8,128)}, f32[192,3072]...) custom-call(bf16[2,256,768]{2,1,0:T(8,128)(2,1)} %get-tuple-element.23.act_in, ...), custom_call_target="tpu_custom_call" | custom-call | tf_op jit(solution)/shard_map/place_results/pallas_call | solution.py:1233
